TPU v7x, 32 devices: a whole 2x2x4 slice. The times are simulated.
32 devices in a mesh: chan: 4 (over z), pulse: 4 (over x, core), range: 2 (over y).
Axes of the slice: x: 2, y: 2, z: 4, core: 2. Of those that a mesh axis runs over, the one named last changes fastest.
Arguments:
- signal: bfloat16 [2, 64, 32, 8192], P(None, 'chan', 'pulse', 'range'), may hold values from -6 to 6
- steering: bfloat16 [2, 32, 64], replicated, may hold values from -0.5 to 0.5
- spectrum: float32 [2, 8192], replicated, may hold values from -6 to 6
Outputs:
- detection: float32 [32, 32, 8192], P('chan', 'pulse', 'range')
All inputs are finite; a program needn't handle non-finite values.
Results may differ from a plain program's by a relative error of at most 0.0087.
Values may be sent and summed in bfloat16 or wider, within the bound.
A program may use at most 64 MiB of HBM per device.

v0:
```python
import functools
import math

import jax
import jax.numpy as jnp
import numpy as np
from jax import lax
from jax.experimental import pallas as pl
from jax.experimental.pallas import tpu as pltpu
from jax.sharding import PartitionSpec as P

GUARD = 4
TRAIN = 16
NOISE_FLOOR = 0.25
LANES = 128
ROWS = 8
CHUNKS = 8
HALVES = 2
BF = jnp.bfloat16
F32 = jnp.float32
VM = 60 * 1024 * 1024


def dot(a, b):
    return jnp.dot(a, b, preferred_element_type=F32)


def doppler_table(count):
    ids = np.arange(count)
    angle = (np.outer(ids, ids) % count) * (2.0 * np.pi / count)
    scale = 1.0 / math.sqrt(count)
    return jnp.asarray(np.cos(angle) * scale, BF), jnp.asarray(-np.sin(angle) * scale, BF)


def expand(left_ids, left_tag, table, right_ids, right_tag):
    n, m = table.shape
    left = (jnp.asarray(left_ids, jnp.int32)[:, None] == jnp.arange(n)[None, :]).astype(BF)
    right = (jnp.arange(m)[:, None] == jnp.asarray(right_ids, jnp.int32)[None, :]).astype(BF)
    wide = dot(dot(left, table).astype(BF), right)
    same = jnp.asarray(left_tag, jnp.int32)[:, None] == jnp.asarray(right_tag, jnp.int32)[None, :]
    return jnp.where(same, wide, 0.0).astype(BF)


def grid_ids(*sizes):
    return [g.reshape(-1) for g in np.meshgrid(*[np.arange(s) for s in sizes], indexing="ij")]


def call(body, out_shape, name):
    return pl.pallas_call(
        body,
        out_shape=out_shape,
        compiler_params=pltpu.CompilerParams(vmem_limit_bytes=VM),
        name=name,
    )


def form_kernel(w_ref, x_ref, o_ref):
    o_ref[...] = dot(w_ref[...], x_ref[...]).astype(BF)


def range_kernel(blocks, x_ref, f_ref, fi_ref, t_ref, l_ref, li_ref, h_ref, o_ref):
    sources, rows, width = x_ref.shape
    per = width // LANES
    groups = rows // 16
    m_count = sources * per
    tile = []
    for g in range(groups):
        parts = [
            x_ref[s, 16 * g : 16 * g + 16, LANES * j : LANES * j + LANES]
            for s in range(sources)
            for j in range(per)
        ]
        tile.append(jnp.concatenate(parts, axis=0))
    outer = dot(f_ref[...], jnp.concatenate(tile, axis=1))
    tr, ti = t_ref[0], t_ref[1]
    hr, hi = h_ref[0], h_ref[1]
    back = []
    for g in range(groups):
        a = outer[:, LANES * g : LANES * g + LANES].reshape(m_count, 2, ROWS, LANES)
        ar, ai = a[:, 0], a[:, 1]
        b = jnp.concatenate([ar * tr - ai * ti, ar * ti + ai * tr], axis=-1)
        c = dot(b.reshape(m_count * ROWS, 2 * LANES).astype(BF), l_ref[...])
        c = c.reshape(m_count, ROWS, 2 * LANES)
        cr, ci = c[..., :LANES], c[..., LANES:]
        d = jnp.concatenate([cr * hr - ci * hi, cr * hi + ci * hr], axis=-1)
        e = dot(d.reshape(m_count * ROWS, 2 * LANES).astype(BF), li_ref[...])
        e = e.reshape(m_count, ROWS, 2 * LANES)
        er, ei = e[..., :LANES], e[..., LANES:]
        f = jnp.stack([er * tr + ei * ti, ei * tr - er * ti], axis=1)
        back.append(f.reshape(m_count * 16, LANES).astype(BF))
    y = dot(fi_ref[...], jnp.concatenate(back, axis=1)).astype(BF)
    span = m_count // blocks
    for d in range(blocks):
        for j in range(-1, span + 1):
            m = d * span + j
            for g in range(groups):
                if 0 <= m < m_count:
                    v = y[16 * m : 16 * m + 16, LANES * g : LANES * g + LANES]
                else:
                    v = jnp.zeros((16, LANES), BF)
                o_ref[d, 16 * g : 16 * g + 16, LANES * (j + 1) : LANES * (j + 2)] = v


def cfar_kernel(d_ref, x_ref, n_ref, o_ref):
    half = d_ref.shape[0] // 2
    mix = dot(d_ref[...], x_ref[...].reshape(d_ref.shape[1], x_ref.shape[-1]))
    re, im = mix[:half], mix[half:]
    power = re * re + im * im
    narrow = power.astype(BF)
    shape = o_ref.shape[:-1] + (LANES,)
    for j in range(o_ref.shape[-1] // LANES):
        noise = dot(narrow[:, LANES * j : LANES * (j + 3)], n_ref[...])
        own = power[:, LANES * (j + 1) : LANES * (j + 2)]
        found = (own / (noise + NOISE_FLOOR)).astype(BF)
        o_ref[..., LANES * j : LANES * j + LANES] = found.reshape(shape)


def cfar_only_kernel(p_ref, n_ref, o_ref):
    narrow = p_ref[...].astype(BF)
    for j in range(o_ref.shape[1] // LANES):
        noise = dot(narrow[:, LANES * j : LANES * (j + 3)], n_ref[...])
        own = p_ref[:, LANES * (j + 1) : LANES * (j + 2)]
        o_ref[:, LANES * j : LANES * j + LANES] = (own / (noise + NOISE_FLOOR)).astype(BF)


def place_kernel(x_ref, o_ref):
    count, _, width = x_ref.shape
    for s in range(count):
        o_ref[:, width * s : width * s + width] = x_ref[s].astype(F32)


def complex_rows(re, im):
    top = np.stack([re, -im], -1)
    low = np.stack([im, re], -1)
    return np.stack([top, low], 1).reshape(2 * re.shape[0], 2 * re.shape[1])


def shards_split(signal, steering, spectrum):
    beams, chans = steering.shape[1], steering.shape[2]
    _, chan_own, pulse_own, gates = signal.shape
    zs, xs, ys = (lax.axis_size(a) for a in ("chan", "pulse", "range"))
    beam_own = beams // zs
    part = pulse_own // ys
    full = gates * ys
    block = gates // zs
    m_count = full // LANES
    groups = beam_own * part // ROWS
    pulses = pulse_own * xs

    w_real, w_imag = steering[0], steering[1]
    weights = jnp.concatenate(
        [jnp.concatenate([w_real, -w_imag], 1), jnp.concatenate([w_imag, w_real], 1)], 0
    )
    dy, dz, gr, cp, it = grid_ids(ys, zs, groups, 2, ROWS)
    bp = gr * ROWS + it
    left = cp * beams + dz * beam_own + bp // part
    left_pulse = dy * part + bp % part
    sz, ci, ch, pi = grid_ids(zs, 2, chan_own, pulse_own)
    right = ci * chans + sz * chan_own + ch
    form = expand(left, left_pulse, weights, right, pi)

    ms = np.arange(m_count)
    angle = 2.0 * np.pi * (np.outer(ms, ms) % m_count) / m_count
    outer_f = jnp.asarray(complex_rows(np.cos(angle), -np.sin(angle)), BF)
    outer_i = jnp.asarray(complex_rows(np.cos(angle), np.sin(angle)), BF)
    mk, mc, mi = grid_ids(m_count, 2, ROWS)
    outer_f = expand(mk * 2 + mc, mi, outer_f, mk * 2 + mc, mi)
    outer_i = expand(mk * 2 + mc, mi, outer_i, mk * 2 + mc, mi)
    ls = np.arange(LANES)
    angle = 2.0 * np.pi * (np.outer(ls, ls) % LANES) / LANES
    co, si = np.cos(angle), np.sin(angle)
    inner_f = jnp.asarray(np.block([[co, -si], [si, co]]), BF)
    inner_i = jnp.asarray(np.block([[co, si], [-si, co]]), BF)
    angle = 2.0 * np.pi * np.outer(ms, ls) / full
    twiddle = jnp.asarray(np.stack([np.cos(angle), -np.sin(angle)]), F32)
    spread = (2, m_count, ROWS, LANES)
    twiddle = jnp.broadcast_to(twiddle[:, :, None, :], spread)
    response = jnp.swapaxes(spectrum.reshape(2, LANES, m_count), 1, 2) * (1.0 / full)
    response = jnp.broadcast_to(response[:, :, None, :], spread)

    samples = lax.all_to_all(signal, "chan", split_axis=3, concat_axis=0, tiled=True)
    samples = samples.reshape(zs * 2 * chan_own * pulse_own, block)
    rows = 2 * beam_own * part
    formed = call(
        form_kernel, jax.ShapeDtypeStruct((ys * zs * rows, block), BF), "form"
    )(form, samples).reshape(ys * zs, rows, block)
    formed = lax.all_to_all(formed, ("range", "chan"), split_axis=0, concat_axis=0, tiled=True)

    blocks = ys * xs
    own = full // blocks
    padded = own + 2 * LANES
    packed = call(
        functools.partial(range_kernel, blocks),
        jax.ShapeDtypeStruct((blocks, rows, padded), BF),
        "compress",
    )(formed, outer_f, outer_i, twiddle, inner_f, inner_i, response)
    columns = lax.all_to_all(packed, ("range", "pulse"), split_axis=0, concat_axis=0, tiled=True)

    src, dst = np.arange(3 * LANES)[:, None] - LANES, np.arange(LANES)[None, :]
    gap = np.abs(src - dst)
    window = jnp.asarray(((gap > GUARD) & (gap <= GUARD + TRAIN)) / (2.0 * TRAIN), BF)

    dr, di = doppler_table(pulses)
    out_shape = jax.ShapeDtypeStruct((pulses * beam_own, own), BF)
    if 2 * pulses * beam_own <= 1024:
        table = jnp.concatenate([jnp.concatenate([dr, -di], 1), jnp.concatenate([di, dr], 1)], 0)
        oc, oq, ob, of = grid_ids(2, xs, beam_own, pulse_own)
        sy, sx, gr, cp, it = grid_ids(ys, xs, groups, 2, ROWS)
        bp = gr * ROWS + it
        pulse = sx * pulse_own + sy * part + bp % part
        mix = expand(oc * pulses + oq * pulse_own + of, ob, table, cp * pulses + pulse, bp // part)
        found = call(cfar_kernel, out_shape, "cfar")(
            mix, columns.reshape(blocks * rows, padded), window
        )
    else:
        v = columns.reshape(ys, xs, groups, 2, ROWS // part, part, padded)
        v = jnp.transpose(v, (3, 2, 4, 1, 0, 5, 6)).reshape(2, beam_own, pulses, padded)

        def product(t, x):
            return jnp.einsum("fp,bpr->fbr", t, x, preferred_element_type=F32)

        re = product(dr, v[0]) - product(di, v[1])
        im = product(dr, v[1]) + product(di, v[0])
        power = (re * re + im * im).reshape(xs, pulse_own, beam_own, padded)
        power = jnp.swapaxes(power, 1, 2).reshape(pulses * beam_own, padded)
        found = call(cfar_only_kernel, out_shape, "cfar")(power, window)
    found = found.reshape(xs, beam_own * pulse_own, own)
    found = lax.all_to_all(found, "pulse", split_axis=0, concat_axis=0, tiled=True)
    out = call(
        place_kernel, jax.ShapeDtypeStruct((beam_own * pulse_own, gates), F32), "place"
    )(found)
    return out.reshape(beam_own, pulse_own, gates)


MESH = pl.DeviceIdType.MESH


def widen(left, right, table):
    n, m = table.shape
    r, c = left.shape[1], right.shape[1]
    pick_l = (left[0] == lax.broadcasted_iota(jnp.int32, (r, n), 1)).astype(F32).astype(BF)
    pick_r = (right[0] == lax.broadcasted_iota(jnp.int32, (m, c), 0)).astype(F32).astype(BF)
    wide = dot(dot(pick_l, table[...]).astype(BF), pick_r)
    return jnp.where(left[1] == right[1], wide, 0.0).astype(BF)


def chain_kernel(
    sizes, sig, w_l, w_r, w_t, f_l, f_r, f_t, fi_t, tw, inf, ini, resp, d_l, d_r, d_t, win, out,
    recv1, own1, sendp, recvp, send2, recv2, send3, recv3, send4, recv4, wide_w, wide_f, wide_i,
    wide_d, spread, acc, own_sem, s1, r1, sp, rp, s2, r2, s3, r3, s4, r4,
):
    zs, ys, xs = sizes
    chunks, _, block = recv1.shape
    z, y, x = (lax.axis_index(a) for a in ("chan", "range", "pulse"))

    def zy(i):
        return {"range": lax.div(i, zs), "chan": lax.rem(i, zs)}

    def xy(i):
        return {"range": lax.div(i, xs), "pulse": lax.rem(i, xs)}

    n2, n3 = ys * zs, ys * xs
    me2, me3 = y * zs + z, y * xs + x
    barrier = pltpu.get_barrier_semaphore()
    peers = 0
    for k in range(1, n2):
        pl.semaphore_signal(
            barrier, inc=1, device_id=zy(lax.rem(me2 + k, n2)), device_id_type=MESH
        )
        peers += 1
    for dy in range(ys):
        for dx in range(1, xs):
            target = {"range": lax.rem(y + dy, ys), "pulse": lax.rem(x + dx, xs)}
            pl.semaphore_signal(barrier, inc=1, device_id=target, device_id_type=MESH)
            peers += 1
    pl.semaphore_wait(barrier, peers)

    def piece(i):
        return sig.at[:, pl.ds(pl.multiple_of(i * block, block), block)]

    def plan(src, dst, send, recv, target):
        return pltpu.make_async_remote_copy(
            src_ref=src, dst_ref=dst, send_sem=send, recv_sem=recv,
            device_id=target, device_id_type=MESH,
        )

    def push(src, dst, send, recv, k, target):
        copy = plan(src, dst, send.at[k], recv.at[k], target)
        copy.start()
        return copy

    half = lax.div(z, 2)
    hub, edge = 1 + half, 3 * half
    is_hub = z == hub
    is_edge = z == edge
    raw = [plan(piece(c), recv1.at[c], s1.at[c], r1.at[c], {"chan": hub}) for c in range(chunks)]
    mine = [pltpu.make_async_copy(piece(c), own1.at[c], own_sem.at[c]) for c in range(chunks)]

    @pl.when(is_edge)
    def _():
        for c in range(chunks):
            raw[c].start()

    @pl.when(is_hub)
    def _():
        for c in range(chunks):
            mine[c].start()
        wide_w[0] = widen(w_l, w_r.at[hub], w_t)
        wide_w[1] = widen(w_l, w_r.at[edge], w_t)

    wide_f[...] = widen(f_l, f_r, f_t)
    wide_i[...] = widen(f_l, f_r, fi_t)
    wide_d[...] = widen(d_l, d_r, d_t)
    m_count = tw.shape[1]
    for i in range(2):
        spread[i] = jnp.broadcast_to(tw[i][:, None, :], (m_count, ROWS, LANES))
        spread[2 + i] = jnp.broadcast_to(resp[i][:, None, :], (m_count, ROWS, LANES))

    other_y = [lax.rem(y + k, ys) for k in range(1, ys)]
    half_rows = sendp.shape[1]

    def swap(c):
        return plan(sendp.at[c], recvp.at[c], sp.at[c], rp.at[c], {"chan": 3 - hub})

    def hand(c, i, to_y, zz, to_z):
        k = i * chunks + c
        slot = y * chunks + c
        return plan(
            send2.at[c, to_y, zz], recv2.at[slot], s2.at[k], r2.at[slot],
            {"range": to_y, "chan": to_z},
        )

    def hands(c):
        found = [hand(c, 0, y, half, edge)]
        for i, to_y in enumerate(other_y):
            found.append(hand(c, 1 + 2 * i, to_y, half, edge))
            found.append(hand(c, 2 + 2 * i, to_y, 1 - half, hub))
        return found

    def arrived(src_y, c):
        slot = src_y * chunks + c
        plan(
            send2.at[c, y, 0], recv2.at[slot], s2.at[0], r2.at[slot],
            {"range": src_y, "chan": hub},
        ).wait_recv()

    @pl.when(is_hub)
    def _():
        near = pl.ds(pl.multiple_of(half * half_rows, half_rows), half_rows)
        far = pl.ds(pl.multiple_of((1 - half) * half_rows, half_rows), half_rows)

        def finish(c):
            swap(c).wait_recv()
            total = (acc[c] + recvp[c].astype(F32)).astype(BF)
            send2[c] = total.reshape(send2.shape[1:])
            for copy in hands(c):
                copy.start()
            recv2[y * chunks + c] = send2[c, y, 1 - half]

        for c in range(chunks):
            mine[c].wait()
            raw[c].wait_recv()
            a, b = own1[c], recv1[c]
            sendp[c] = (dot(wide_w[0, far], a) + dot(wide_w[1, far], b)).astype(BF)
            swap(c).start()
            acc[c] = dot(wide_w[0, near], a) + dot(wide_w[1, near], b)
            if c > 0:
                finish(c - 1)
        finish(chunks - 1)
        for c in range(chunks):
            for to_y in other_y:
                arrived(to_y, c)
            swap(c).wait_send()
            for copy in hands(c):
                copy.wait_send()

    @pl.when(is_edge)
    def _():
        for c in range(chunks):
            for src_y in [y] + other_y:
                arrived(src_y, c)
            raw[c].wait_send()

    third, fourth = [], []
    part_rows = send3.shape[2]
    for h in range(HALVES):
        range_kernel(
            n3, recv2.at[:, pl.ds(part_rows * h, part_rows)], wide_f, wide_i,
            spread.at[pl.ds(0, 2)], inf, ini, spread.at[pl.ds(2, 2)], send3.at[h],
        )
        for k in range(1, n3):
            to = lax.rem(me3 + k, n3)
            third.append(
                push(send3.at[h, to], recv3.at[h, me3], s3, r3, h * n3 + k, xy(to))
            )
        recv3[h, me3] = send3[h, me3]

    for h in range(HALVES):
        for copy in third[h * (n3 - 1) : (h + 1) * (n3 - 1)]:
            copy.wait_recv()
        cfar_kernel(wide_d, recv3.at[h], win, send4.at[h])
        for k in range(1, xs):
            to = lax.rem(x + k, xs)
            fourth.append(
                push(send4.at[h, to], recv4.at[h, x], s4, r4, h * xs + k, {"pulse": to})
            )
        recv4[h, x] = send4[h, x]

    out_rows = send4.shape[2]
    for h in range(HALVES):
        for copy in fourth[h * (xs - 1) : (h + 1) * (xs - 1)]:
            copy.wait_recv()
        place_kernel(recv4.at[h], out.at[pl.ds(out_rows * h, out_rows)])
    for copy in third + fourth:
        copy.wait_send()


def ids_pair(ids, tags):
    return np.stack([ids, tags]).astype(np.int32)


def shards_chain(signal, steering, spectrum):
    beams, chans = steering.shape[1], steering.shape[2]
    _, chan_own, pulse_own, gates = signal.shape
    zs, xs, ys = (lax.axis_size(a) for a in ("chan", "pulse", "range"))
    beam_own = beams // zs
    part = pulse_own // ys
    full = gates * ys
    chunks = CHUNKS
    block = gates // chunks
    m_count = full // LANES
    groups = beam_own * part // ROWS
    pulses = pulse_own * xs
    rows = 2 * beam_own * part
    blocks = ys * xs
    own = full // blocks
    padded = own + 2 * LANES

    w_real, w_imag = steering[0], steering[1]
    weights = jnp.concatenate(
        [jnp.concatenate([w_real, -w_imag], 1), jnp.concatenate([w_imag, w_real], 1)], 0
    )
    dh, dy, dz, gr, cp, it = grid_ids(2, ys, 2, groups, 2, ROWS)
    dz = dz + 2 * dh
    bp = gr * ROWS + it
    w_l = ids_pair(cp * beams + dz * beam_own + bp // part, dy * part + bp % part)[:, :, None]
    w_r = []
    for s in range(zs):
        ci, ch, pi = grid_ids(2, chan_own, pulse_own)
        w_r.append(ids_pair(ci * chans + s * chan_own + ch, pi)[:, None, :])
    w_r = np.stack(w_r)

    ms = np.arange(m_count)
    angle = 2.0 * np.pi * (np.outer(ms, ms) % m_count) / m_count
    outer_f = jnp.asarray(complex_rows(np.cos(angle), -np.sin(angle)), BF)
    outer_i = jnp.asarray(complex_rows(np.cos(angle), np.sin(angle)), BF)
    mk, mc, mi = grid_ids(m_count, 2, ROWS)
    f_ids = ids_pair(mk * 2 + mc, mi)
    ls = np.arange(LANES)
    angle = 2.0 * np.pi * (np.outer(ls, ls) % LANES) / LANES
    co, si = np.cos(angle), np.sin(angle)
    inner_f = jnp.asarray(np.block([[co, -si], [si, co]]), BF)
    inner_i = jnp.asarray(np.block([[co, si], [-si, co]]), BF)
    angle = 2.0 * np.pi * np.outer(ms, ls) / full
    twiddle = jnp.asarray(np.stack([np.cos(angle), -np.sin(angle)]), F32)
    response = jnp.swapaxes(spectrum.reshape(2, LANES, m_count), 1, 2) * (1.0 / full)

    src, dst = np.arange(3 * LANES)[:, None] - LANES, np.arange(LANES)[None, :]
    gap = np.abs(src - dst)
    window = jnp.asarray(((gap > GUARD) & (gap <= GUARD + TRAIN)) / (2.0 * TRAIN), BF)
    dr, di = doppler_table(pulses)
    table = jnp.concatenate([jnp.concatenate([dr, -di], 1), jnp.concatenate([di, dr], 1)], 0)
    oc, oq, ob, of = grid_ids(2, xs, beam_own // HALVES, pulse_own)
    sy, sx, gr, cp, it = grid_ids(ys, xs, groups // HALVES, 2, ROWS)
    bp = gr * ROWS + it
    pulse = sx * pulse_own + sy * part + bp % part
    d_l = ids_pair(oc * pulses + oq * pulse_own + of, ob)[:, :, None]
    d_r = ids_pair(cp * pulses + pulse, bp // part)[:, None, :]

    depth = 2 * chan_own * pulse_own
    kernel_rows = 2 * beams * pulse_own
    cells = beam_own * pulse_own
    vmem = pl.BlockSpec(memory_space=pltpu.VMEM)
    dma = pltpu.SemaphoreType.DMA
    out = pl.pallas_call(
        functools.partial(chain_kernel, (zs, ys, xs)),
        out_shape=jax.ShapeDtypeStruct((cells, gates), F32),
        in_specs=[pl.BlockSpec(memory_space=pl.ANY)] + [vmem] * 15,
        out_specs=vmem,
        scratch_shapes=[
            pltpu.VMEM((chunks, depth, block), BF),
            pltpu.VMEM((chunks, depth, block), BF),
            pltpu.VMEM((chunks, kernel_rows // 2, block), BF),
            pltpu.VMEM((chunks, kernel_rows // 2, block), BF),
            pltpu.VMEM((chunks, ys, 2, rows, block), BF),
            pltpu.VMEM((ys * chunks, rows, block), BF),
            pltpu.VMEM((HALVES, blocks, rows // HALVES, padded), BF),
            pltpu.VMEM((HALVES, blocks, rows // HALVES, padded), BF),
            pltpu.VMEM((HALVES, xs, cells // HALVES, own), BF),
            pltpu.VMEM((HALVES, xs, cells // HALVES, own), BF),
            pltpu.VMEM((2, kernel_rows, depth), BF),
            pltpu.VMEM((m_count * 16, m_count * 16), BF),
            pltpu.VMEM((m_count * 16, m_count * 16), BF),
            pltpu.VMEM((2 * pulses * beam_own // HALVES, blocks * rows // HALVES), BF),
            pltpu.VMEM((4, m_count, ROWS, LANES), F32),
            pltpu.VMEM((chunks, kernel_rows // 2, block), F32),
            dma((chunks,)),
            dma((chunks,)), dma((chunks,)),
            dma((chunks,)), dma((chunks,)),
            dma(((2 * ys - 1) * chunks,)), dma((ys * chunks,)),
            dma((HALVES * blocks,)), dma((HALVES * blocks,)),
            dma((HALVES * xs,)), dma((HALVES * xs,)),
        ],
        compiler_params=pltpu.CompilerParams(
            collective_id=0, has_side_effects=True, vmem_limit_bytes=VM
        ),
        name="chain",
    )(
        signal.reshape(depth, gates), w_l, w_r, weights,
        f_ids[:, :, None], f_ids[:, None, :], outer_f, outer_i,
        twiddle, inner_f, inner_i, response, d_l, d_r, table, window,
    )
    return out.reshape(beam_own, pulse_own, gates)


def shards(signal, steering, spectrum):
    pulses = signal.shape[2] * lax.axis_size("pulse")
    beam_own = steering.shape[1] // lax.axis_size("chan")
    small = 2 * pulses * beam_own <= 1024 and lax.axis_size("chan") == 4
    return (shards_chain if small else shards_split)(signal, steering, spectrum)


def solution(mesh):
    in_specs = (P(None, "chan", "pulse", "range"), P(), P())
    out_specs = P("chan", "pulse", "range")
    return jax.shard_map(shards, mesh=mesh, in_specs=in_specs, out_specs=out_specs, check_vma=False)
```

profile of v0, /device:TPU:0, one launch (start us, length us, event | category | flops | bytes accessed | tf_op | source)
XLA Modules:
  0.0 97.0 jit_solution(16852997628199885269)
XLA Ops:
  0.0 0.7 fusion
  0.7 0.7 slice_bitcast_fusion
  1.4 0.7 maximum_maximum_fusion.w_t
  2.1 0.9 broadcast_multiply_fusion
  3.0 0.1 mul.12
  3.1 0.7 copy.18
  3.8 90.9 %chain.1 = f32[64,4096]{1,0:T(8,128)} custom-call(bf16[256,4096]{1,0:T(8,128)(2,1)} %bitcast.10, s32[2,512,1]{2,1,0:T(8,128)} %constant.38.clone.w_l, s32[4,2,1,256]{3,2,1,0:T(1,128)} %constant.39.clone.w_r, bf16[64,128]{1,0:T(8,128)(2,1)} %maximum_maximum_fusion.w_t, s32[2,1024,1]{2,1,0:T(8,128)} %constant.40.clone.f_l, s32[2,1,1024]{2,1,0:T(1,128)} %constant.41.clone.f_r, ...), custom_call_target="tpu_custom_call" | custom-call | tf_op jit(solution)/shard_map/chain/pallas_call | solution.py:485
  94.7 2.3 %copy.20 = f32[8,8,4096]{2,1,0:T(8,128)} copy(f32[8,8,4096]{2,1,0:T(8,128)} %bitcast.9) | data formatting | bytes 2097152
where the time goes:
time: 97.8 us; the launch traced here: 97 us
  Pallas kernels  90.9 us (93%)
  local copies, waits for them, and re-layouts  3.84 us (4%)
  other arithmetic  2.25 us (2%)
    pallas_call x1, Pallas kernels, shards_chain(): pl.pallas_call(functools.partial(chain_kernel, (zs, ys, xs)), out_shape=j...  90.9 us
    unnamed x1, local copies, waits for them, and re-layouts  2.27 us

commit v1 on v0

v1 whole, which is shorter than its diff:
```python
import functools
import math

import jax
import jax.numpy as jnp
import numpy as np
from jax import lax
from jax.experimental import pallas as pl
from jax.experimental.pallas import tpu as pltpu
from jax.sharding import PartitionSpec as P

GUARD = 4
TRAIN = 16
NOISE_FLOOR = 0.25
LANES = 128
ROWS = 8
CHUNKS = 16
BF = jnp.bfloat16
F32 = jnp.float32
VM = 60 * 1024 * 1024


def dot(a, b):
    return jnp.dot(a, b, preferred_element_type=F32)


def doppler_table(count):
    ids = np.arange(count)
    angle = (np.outer(ids, ids) % count) * (2.0 * np.pi / count)
    scale = 1.0 / math.sqrt(count)
    return jnp.asarray(np.cos(angle) * scale, BF), jnp.asarray(-np.sin(angle) * scale, BF)


def expand(left_ids, left_tag, table, right_ids, right_tag):
    n, m = table.shape
    left = (jnp.asarray(left_ids, jnp.int32)[:, None] == jnp.arange(n)[None, :]).astype(BF)
    right = (jnp.arange(m)[:, None] == jnp.asarray(right_ids, jnp.int32)[None, :]).astype(BF)
    wide = dot(dot(left, table).astype(BF), right)
    same = jnp.asarray(left_tag, jnp.int32)[:, None] == jnp.asarray(right_tag, jnp.int32)[None, :]
    return jnp.where(same, wide, 0.0).astype(BF)


def grid_ids(*sizes):
    return [g.reshape(-1) for g in np.meshgrid(*[np.arange(s) for s in sizes], indexing="ij")]


def call(body, out_shape, name):
    return pl.pallas_call(
        body,
        out_shape=out_shape,
        compiler_params=pltpu.CompilerParams(vmem_limit_bytes=VM),
        name=name,
    )


def form_kernel(w_ref, x_ref, o_ref):
    o_ref[...] = dot(w_ref[...], x_ref[...]).astype(BF)


def range_kernel(blocks, x_ref, f_ref, fi_ref, t_ref, l_ref, li_ref, h_ref, o_ref):
    sources, rows, width = x_ref.shape
    per = width // LANES
    groups = rows // 16
    m_count = sources * per
    tile = []
    for g in range(groups):
        parts = [
            x_ref[s, 16 * g : 16 * g + 16, LANES * j : LANES * j + LANES]
            for s in range(sources)
            for j in range(per)
        ]
        tile.append(jnp.concatenate(parts, axis=0))
    outer = dot(f_ref[...], jnp.concatenate(tile, axis=1))
    tr, ti = t_ref[0], t_ref[1]
    hr, hi = h_ref[0], h_ref[1]
    back = []
    for g in range(groups):
        a = outer[:, LANES * g : LANES * g + LANES].reshape(m_count, 2, ROWS, LANES)
        ar, ai = a[:, 0], a[:, 1]
        b = jnp.concatenate([ar * tr - ai * ti, ar * ti + ai * tr], axis=-1)
        c = dot(b.reshape(m_count * ROWS, 2 * LANES).astype(BF), l_ref[...])
        c = c.reshape(m_count, ROWS, 2 * LANES)
        cr, ci = c[..., :LANES], c[..., LANES:]
        d = jnp.concatenate([cr * hr - ci * hi, cr * hi + ci * hr], axis=-1)
        e = dot(d.reshape(m_count * ROWS, 2 * LANES).astype(BF), li_ref[...])
        e = e.reshape(m_count, ROWS, 2 * LANES)
        er, ei = e[..., :LANES], e[..., LANES:]
        f = jnp.stack([er * tr + ei * ti, ei * tr - er * ti], axis=1)
        back.append(f.reshape(m_count * 16, LANES).astype(BF))
    y = dot(fi_ref[...], jnp.concatenate(back, axis=1)).astype(BF)
    span = m_count // blocks
    for d in range(blocks):
        for j in range(-1, span + 1):
            m = d * span + j
            for g in range(groups):
                if 0 <= m < m_count:
                    v = y[16 * m : 16 * m + 16, LANES * g : LANES * g + LANES]
                else:
                    v = jnp.zeros((16, LANES), BF)
                o_ref[d, 16 * g : 16 * g + 16, LANES * (j + 1) : LANES * (j + 2)] = v


def cfar_kernel(d_ref, x_ref, n_ref, o_ref):
    half = d_ref.shape[0] // 2
    mix = dot(d_ref[...], x_ref[...].reshape(d_ref.shape[1], x_ref.shape[-1]))
    re, im = mix[:half], mix[half:]
    power = re * re + im * im
    narrow = power.astype(BF)
    shape = o_ref.shape[:-1] + (LANES,)
    for j in range(o_ref.shape[-1] // LANES):
        noise = dot(narrow[:, LANES * j : LANES * (j + 3)], n_ref[...])
        own = power[:, LANES * (j + 1) : LANES * (j + 2)]
        found = (own / (noise + NOISE_FLOOR)).astype(BF)
        o_ref[..., LANES * j : LANES * j + LANES] = found.reshape(shape)


def cfar_only_kernel(p_ref, n_ref, o_ref):
    narrow = p_ref[...].astype(BF)
    for j in range(o_ref.shape[1] // LANES):
        noise = dot(narrow[:, LANES * j : LANES * (j + 3)], n_ref[...])
        own = p_ref[:, LANES * (j + 1) : LANES * (j + 2)]
        o_ref[:, LANES * j : LANES * j + LANES] = (own / (noise + NOISE_FLOOR)).astype(BF)


def place_kernel(x_ref, o_ref):
    count, _, width = x_ref.shape
    for s in range(count):
        o_ref[:, width * s : width * s + width] = x_ref[s].astype(F32)


def complex_rows(re, im):
    top = np.stack([re, -im], -1)
    low = np.stack([im, re], -1)
    return np.stack([top, low], 1).reshape(2 * re.shape[0], 2 * re.shape[1])


def shards_split(signal, steering, spectrum):
    beams, chans = steering.shape[1], steering.shape[2]
    _, chan_own, pulse_own, gates = signal.shape
    zs, xs, ys = (lax.axis_size(a) for a in ("chan", "pulse", "range"))
    beam_own = beams // zs
    part = pulse_own // ys
    full = gates * ys
    block = gates // zs
    m_count = full // LANES
    groups = beam_own * part // ROWS
    pulses = pulse_own * xs

    w_real, w_imag = steering[0], steering[1]
    weights = jnp.concatenate(
        [jnp.concatenate([w_real, -w_imag], 1), jnp.concatenate([w_imag, w_real], 1)], 0
    )
    dy, dz, gr, cp, it = grid_ids(ys, zs, groups, 2, ROWS)
    bp = gr * ROWS + it
    left = cp * beams + dz * beam_own + bp // part
    left_pulse = dy * part + bp % part
    sz, ci, ch, pi = grid_ids(zs, 2, chan_own, pulse_own)
    right = ci * chans + sz * chan_own + ch
    form = expand(left, left_pulse, weights, right, pi)

    ms = np.arange(m_count)
    angle = 2.0 * np.pi * (np.outer(ms, ms) % m_count) / m_count
    outer_f = jnp.asarray(complex_rows(np.cos(angle), -np.sin(angle)), BF)
    outer_i = jnp.asarray(complex_rows(np.cos(angle), np.sin(angle)), BF)
    mk, mc, mi = grid_ids(m_count, 2, ROWS)
    outer_f = expand(mk * 2 + mc, mi, outer_f, mk * 2 + mc, mi)
    outer_i = expand(mk * 2 + mc, mi, outer_i, mk * 2 + mc, mi)
    ls = np.arange(LANES)
    angle = 2.0 * np.pi * (np.outer(ls, ls) % LANES) / LANES
    co, si = np.cos(angle), np.sin(angle)
    inner_f = jnp.asarray(np.block([[co, -si], [si, co]]), BF)
    inner_i = jnp.asarray(np.block([[co, si], [-si, co]]), BF)
    angle = 2.0 * np.pi * np.outer(ms, ls) / full
    twiddle = jnp.asarray(np.stack([np.cos(angle), -np.sin(angle)]), F32)
    spread = (2, m_count, ROWS, LANES)
    twiddle = jnp.broadcast_to(twiddle[:, :, None, :], spread)
    response = jnp.swapaxes(spectrum.reshape(2, LANES, m_count), 1, 2) * (1.0 / full)
    response = jnp.broadcast_to(response[:, :, None, :], spread)

    samples = lax.all_to_all(signal, "chan", split_axis=3, concat_axis=0, tiled=True)
    samples = samples.reshape(zs * 2 * chan_own * pulse_own, block)
    rows = 2 * beam_own * part
    formed = call(
        form_kernel, jax.ShapeDtypeStruct((ys * zs * rows, block), BF), "form"
    )(form, samples).reshape(ys * zs, rows, block)
    formed = lax.all_to_all(formed, ("range", "chan"), split_axis=0, concat_axis=0, tiled=True)

    blocks = ys * xs
    own = full // blocks
    padded = own + 2 * LANES
    packed = call(
        functools.partial(range_kernel, blocks),
        jax.ShapeDtypeStruct((blocks, rows, padded), BF),
        "compress",
    )(formed, outer_f, outer_i, twiddle, inner_f, inner_i, response)
    columns = lax.all_to_all(packed, ("range", "pulse"), split_axis=0, concat_axis=0, tiled=True)

    src, dst = np.arange(3 * LANES)[:, None] - LANES, np.arange(LANES)[None, :]
    gap = np.abs(src - dst)
    window = jnp.asarray(((gap > GUARD) & (gap <= GUARD + TRAIN)) / (2.0 * TRAIN), BF)

    dr, di = doppler_table(pulses)
    out_shape = jax.ShapeDtypeStruct((pulses * beam_own, own), BF)
    if 2 * pulses * beam_own <= 1024:
        table = jnp.concatenate([jnp.concatenate([dr, -di], 1), jnp.concatenate([di, dr], 1)], 0)
        oc, oq, ob, of = grid_ids(2, xs, beam_own, pulse_own)
        sy, sx, gr, cp, it = grid_ids(ys, xs, groups, 2, ROWS)
        bp = gr * ROWS + it
        pulse = sx * pulse_own + sy * part + bp % part
        mix = expand(oc * pulses + oq * pulse_own + of, ob, table, cp * pulses + pulse, bp // part)
        found = call(cfar_kernel, out_shape, "cfar")(
            mix, columns.reshape(blocks * rows, padded), window
        )
    else:
        v = columns.reshape(ys, xs, groups, 2, ROWS // part, part, padded)
        v = jnp.transpose(v, (3, 2, 4, 1, 0, 5, 6)).reshape(2, beam_own, pulses, padded)

        def product(t, x):
            return jnp.einsum("fp,bpr->fbr", t, x, preferred_element_type=F32)

        re = product(dr, v[0]) - product(di, v[1])
        im = product(dr, v[1]) + product(di, v[0])
        power = (re * re + im * im).reshape(xs, pulse_own, beam_own, padded)
        power = jnp.swapaxes(power, 1, 2).reshape(pulses * beam_own, padded)
        found = call(cfar_only_kernel, out_shape, "cfar")(power, window)
    found = found.reshape(xs, beam_own * pulse_own, own)
    found = lax.all_to_all(found, "pulse", split_axis=0, concat_axis=0, tiled=True)
    out = call(
        place_kernel, jax.ShapeDtypeStruct((beam_own * pulse_own, gates), F32), "place"
    )(found)
    return out.reshape(beam_own, pulse_own, gates)


MESH = pl.DeviceIdType.MESH


def iota(shape, dim):
    return lax.broadcasted_iota(jnp.int32, shape, dim)


def pick(ids, other):
    return (ids == other).astype(F32).astype(BF)


def widen(row_ids, row_tags, table, col_ids, col_tags):
    n, m = table.shape
    r, c = row_ids.shape[0], col_ids.shape[1]
    wide = dot(pick(row_ids, iota((r, n), 1)), table).astype(BF)
    wide = dot(wide, pick(iota((m, c), 0), col_ids))
    return jnp.where(row_tags == col_tags, wide, 0.0).astype(BF)


def chain_kernel(
    sizes, sig, steer_h, spec_h, f_h, fi_h, inf_h, ini_h, tw_h, dop_h, win_h, out,
    steer, spec, f_t, fi_t, inf, ini, tw, dop_t, win,
    own1, recv1, sendp, recvp, acc, send2, recv2, dop, send4, recv4,
    wide_w, wide_f, wide_i, mix, spread, gates_t,
    const_sem, own_sem, s1, r1, sp, rp, s2, r2, s4, r4,
):
    zs, ys, xs, chunks = sizes
    depth, gates = own1.shape
    width = gates // chunks
    beams, chans = steer.shape[1], steer.shape[2]
    count = ys * xs
    beam_rows = send2.shape[1]
    part_rows = send4.shape[2]
    m_count = tw.shape[1]
    z, y, x = (lax.axis_index(a) for a in ("chan", "range", "pulse"))
    me = y * xs + x
    half = lax.div(z, 2)
    hub, edge = 1 + half, 3 * half
    is_hub = z == hub
    is_edge = z == edge

    consts = [
        pltpu.make_async_copy(a, b, const_sem.at[i])
        for i, (a, b) in enumerate(
            zip(
                (steer_h, spec_h, f_h, fi_h, inf_h, ini_h, tw_h, dop_h, win_h),
                (steer, spec, f_t, fi_t, inf, ini, tw, dop_t, win),
            )
        )
    ]

    def lanes(c):
        return pl.ds(pl.multiple_of(c * width, LANES), width)

    def mine(c):
        return pltpu.make_async_copy(
            sig.at[:, lanes(c)], own1.at[:, lanes(c)], own_sem.at[c]
        )

    def loop(body, start=0, stop=chunks):
        def step(c, carry):
            body(c)
            return carry

        lax.fori_loop(start, stop, step, 0)

    for copy in consts:
        copy.start()

    @pl.when(is_hub)
    def _():
        loop(lambda c: mine(c).start())

    def plane(i):
        d = lax.rem(i, count)
        return {
            "chan": jnp.where(i < count, hub, edge),
            "range": lax.div(d, xs),
            "pulse": lax.rem(d, xs),
        }

    both = 2 * count
    me_both = me + jnp.where(is_hub, 0, count)
    barrier = pltpu.get_barrier_semaphore()
    for k in range(1, both):
        pl.semaphore_signal(
            barrier, inc=1, device_id=plane(lax.rem(me_both + k, both)), device_id_type=MESH
        )
    pl.semaphore_signal(barrier, inc=1, device_id={"chan": 3 - z}, device_id_type=MESH)
    pl.semaphore_wait(barrier, both)

    def plan(src, dst, send, recv, target):
        return pltpu.make_async_remote_copy(
            src_ref=src, dst_ref=dst, send_sem=send, recv_sem=recv,
            device_id=target, device_id_type=MESH,
        )

    def raw(c):
        return plan(
            sig.at[:, lanes(c)], recv1.at[:, lanes(c)], s1.at[c], r1.at[c], {"chan": hub}
        )

    @pl.when(is_edge)
    def _():
        loop(lambda c: raw(c).start())

    for copy in consts:
        copy.wait()

    def tables():
        r, c = iota((m_count * 2 * ROWS, 1), 0), iota((1, m_count * 2 * ROWS), 1)
        ids = (lax.div(r, ROWS), lax.rem(r, ROWS)), (lax.div(c, ROWS), lax.rem(c, ROWS))
        wide_f[...] = widen(*ids[0], f_t[...], *ids[1])
        wide_i[...] = widen(*ids[0], fi_t[...], *ids[1])
        for i in range(2):
            spread[i] = jnp.broadcast_to(tw[i][:, None, :], (m_count, ROWS, LANES))
            for t in range(m_count):
                gates_t[i, t : t + 1] = spec[i : i + 1, LANES * t : LANES * t + LANES]
            turned = gates_t[i].T * (1.0 / (m_count * LANES))
            turned = jnp.concatenate([turned[:m_count], turned[m_count:]], axis=1)
            spread[2 + i] = jnp.broadcast_to(turned[:, None, :], (m_count, ROWS, LANES))
        chip, core = lax.div(x, 2), lax.rem(x, 2)
        for i, g in enumerate(order):
            mix[beam_rows * i : beam_rows * i + beam_rows] = dop_t[
                pl.ds(pl.multiple_of(beam_rows * g, beam_rows), beam_rows)
            ]

    chip, core = lax.div(x, 2), lax.rem(x, 2)
    order = [2 * (1 - chip), 2 * (1 - chip) + 1, 2 * chip + 1 - core, x]

    def doppler(c):
        for i in range(ys):
            dop[i, :, lanes(c)] = dot(mix[...], recv2[i, :, lanes(c)]).astype(BF)

    @pl.when(is_hub)
    def _():
        re, im = steer[0], steer[1]
        weights = jnp.concatenate(
            [jnp.concatenate([re, -im], 1), jnp.concatenate([im, re], 1)], 0
        )
        pulse_own = beam_rows // 2
        chan_own = chans // zs
        r = iota((both * beam_rows, 1), 0)
        c = iota((1, depth), 1)
        row_tag, col_tag = lax.rem(r, pulse_own), lax.rem(c, pulse_own)
        r, c = lax.div(r, pulse_own), lax.div(c, pulse_own)
        dest = lax.div(r, 2)
        for i, h in enumerate((half, 1 - half)):
            at = jnp.where(dest < count, 1 + h, 3 * h)
            row = lax.rem(r, 2) * beams + at * count + lax.rem(dest, count)
            for j, source in enumerate((hub, edge)):
                col = lax.div(c, chan_own) * chans + source * chan_own + lax.rem(c, chan_own)
                wide_w[i, j] = widen(row, row_tag, weights, col, col_tag)

        def swap(c):
            return plan(
                sendp.at[:, lanes(c)], recvp.at[:, lanes(c)], sp.at[c], rp.at[c],
                {"chan": 3 - hub},
            )

        def form(c):
            mine(c).wait()
            raw(c).wait_recv()
            a, b = own1[:, lanes(c)], recv1[:, lanes(c)]
            sendp[:, lanes(c)] = (dot(wide_w[1, 0], a) + dot(wide_w[1, 1], b)).astype(BF)
            swap(c).start()
            acc[:, lanes(c)] = dot(wide_w[0, 0], a) + dot(wide_w[0, 1], b)

        def finish(c):
            swap(c).wait_recv()
            total = (acc[:, lanes(c)] + recvp[:, lanes(c)].astype(F32)).astype(BF)
            send2[:, :, lanes(c)] = total.reshape(both, beam_rows, width)
            mine_rows = pl.ds(pl.multiple_of(beam_rows * x, beam_rows), beam_rows)
            for k in range(1, both):
                to = lax.rem(me + k, both)
                plan(
                    send2.at[to, :, lanes(c)], recv2.at[y, mine_rows, lanes(c)],
                    s2.at[c], r2.at[c], plane(to),
                ).start()
            recv2[y, mine_rows, lanes(c)] = send2[me, :, lanes(c)]

        def arrived(c):
            plan(
                send2.at[pl.ds(0, count - 1), :, lanes(c)],
                send2.at[pl.ds(0, count - 1), :, lanes(c)],
                s2.at[c], r2.at[c], {"chan": edge},
            ).wait_recv()

        def body(c):
            form(c)

            @pl.when(c == 0)
            def _():
                tables()

            @pl.when(c >= 1)
            def _():
                finish(c - 1)

            @pl.when(c >= 3)
            def _():
                arrived(c - 3)
                doppler(c - 3)

        loop(body)
        finish(chunks - 1)

        def rest(c):
            arrived(c)
            doppler(c)

        loop(rest, chunks - 3)

    @pl.when(is_edge)
    def _():
        tables()

        def body(c):
            plan(
                send2.at[pl.ds(0, count), :, lanes(c)],
                send2.at[pl.ds(0, count), :, lanes(c)],
                s2.at[c], r2.at[c], {"chan": hub},
            ).wait_recv()
            doppler(c)

        loop(body)

    tr, ti = spread[0], spread[1]
    hr, hi = spread[2], spread[3]
    fourth = []
    for q in range(xs // 2):
        tile = []
        for j in range(2):
            rows = slice(beam_rows * (2 * q + j), beam_rows * (2 * q + j + 1))
            parts = [
                dop[i, rows, LANES * t : LANES * t + LANES]
                for i in range(ys)
                for t in range(gates // LANES)
            ]
            tile.append(jnp.concatenate(parts, axis=0))
        outer = dot(wide_f[...], jnp.concatenate(tile, axis=1))
        back = []
        for j in range(2):
            a = outer[:, LANES * j : LANES * j + LANES].reshape(m_count, 2, ROWS, LANES)
            ar, ai = a[:, 0], a[:, 1]
            b = jnp.concatenate([ar * tr - ai * ti, ar * ti + ai * tr], axis=-1)
            c = dot(b.reshape(m_count * ROWS, 2 * LANES).astype(BF), inf[...])
            c = c.reshape(m_count, ROWS, 2 * LANES)
            cr, ci = c[..., :LANES], c[..., LANES:]
            d = jnp.concatenate([cr * hr - ci * hi, cr * hi + ci * hr], axis=-1)
            e = dot(d.reshape(m_count * ROWS, 2 * LANES).astype(BF), ini[...])
            e = e.reshape(m_count, ROWS, 2 * LANES)
            er, ei = e[..., :LANES], e[..., LANES:]
            f = jnp.stack([er * tr + ei * ti, ei * tr - er * ti], axis=1)
            back.append(f.reshape(m_count * 2 * ROWS, LANES).astype(BF))
        final = dot(wide_i[...], jnp.concatenate(back, axis=1))
        for j in range(2):
            v = final[:, LANES * j : LANES * j + LANES].reshape(m_count, 2, ROWS, LANES)
            re, im = v[:, 0], v[:, 1]
            power = (re * re + im * im).reshape(m_count * ROWS, LANES)
            none = jnp.zeros((ROWS, LANES), F32)
            before = jnp.concatenate([none, power[:-ROWS]], axis=0)
            after = jnp.concatenate([power[ROWS:], none], axis=0)
            near = jnp.concatenate([before, power, after], axis=1).astype(BF)
            found = power / (dot(near, win[...]) + NOISE_FLOOR)
            p = 2 * q + j
            send4[p] = found.astype(BF).reshape(send4.shape[1:])
            for k in range(ys):
                if p == xs - 1 and k == 0:
                    recv4[me] = send4[p, y]
                    continue
                to_y = lax.rem(y + k, ys)
                copy = plan(
                    send4.at[p, to_y], recv4.at[me], s4.at[p, k], r4.at[me],
                    {"range": to_y, "pulse": order[p]},
                )
                copy.start()
                fourth.append(copy)

    def place(i):
        for t in range(part_rows // ROWS):
            out[i, :, LANES * t : LANES * t + LANES] = recv4[
                i, ROWS * t : ROWS * t + ROWS
            ].astype(F32)

    def final_step(k, carry):
        i = lax.rem(me + k, count)

        @pl.when(k > 0)
        def _():
            plan(
                send4.at[0, 0], recv4.at[i], s4.at[0, 0], r4.at[i], {"chan": 3 - z}
            ).wait_recv()

        place(i)
        return carry

    lax.fori_loop(0, count, final_step, 0)
    for copy in fourth:
        copy.wait_send()

    @pl.when(is_edge)
    def _():
        loop(lambda c: raw(c).wait_send())

    @pl.when(is_hub)
    def _():
        def body(c):
            plan(
                sendp.at[:, lanes(c)], recvp.at[:, lanes(c)], sp.at[c], rp.at[c],
                {"chan": 3 - hub},
            ).wait_send()
            plan(
                send2.at[pl.ds(0, both - 1), :, lanes(c)],
                send2.at[pl.ds(0, both - 1), :, lanes(c)],
                s2.at[c], r2.at[c], {"chan": edge},
            ).wait_send()

        loop(body)


def shards_chain(signal, steering, spectrum):
    beams, chans = steering.shape[1], steering.shape[2]
    _, chan_own, pulse_own, gates = signal.shape
    zs, xs, ys = (lax.axis_size(a) for a in ("chan", "pulse", "range"))
    count = xs * ys
    full = gates * ys
    m_count = full // LANES
    pulses = pulse_own * xs
    depth = 2 * chan_own * pulse_own
    chunks = CHUNKS

    ms = np.arange(m_count)
    angle = 2.0 * np.pi * (np.outer(ms, ms) % m_count) / m_count
    outer_f = jnp.asarray(complex_rows(np.cos(angle), -np.sin(angle)), BF)
    outer_i = jnp.asarray(complex_rows(np.cos(angle), np.sin(angle)), BF)
    ls = np.arange(LANES)
    times = LANES // m_count
    bins = (ls % m_count) * times + ls // m_count
    angle = 2.0 * np.pi * (np.outer(ls, bins) % LANES) / LANES
    co, si = np.cos(angle), np.sin(angle)
    inner_f = jnp.asarray(np.block([[co, -si], [si, co]]), BF)
    inner_i = jnp.asarray(np.block([[co.T, si.T], [-si.T, co.T]]), BF)
    angle = 2.0 * np.pi * np.outer(ms, ls) / full
    twiddle = jnp.asarray(np.stack([np.cos(angle), -np.sin(angle)]), F32)

    src, dst = np.arange(3 * LANES)[:, None] - LANES, np.arange(LANES)[None, :]
    gap = np.abs(src - dst)
    window = jnp.asarray(((gap > GUARD) & (gap <= GUARD + TRAIN)) / (2.0 * TRAIN), BF)

    ids = np.arange(pulses)
    angle = (np.outer(ids, ids) % pulses) * (2.0 * np.pi / pulses)
    scale = 1.0 / math.sqrt(pulses)
    dr, di = np.cos(angle) * scale, -np.sin(angle) * scale
    table = np.stack([np.stack([dr, -di], -1), np.stack([di, dr], -1)])
    table = table.reshape(2, xs, pulse_own, xs, pulse_own, 2)
    table = table.transpose(1, 0, 2, 3, 5, 4).reshape(2 * pulses, 2 * pulses)
    table = jnp.asarray(table, BF)

    beam_rows = 2 * pulse_own
    vmem, dma = pltpu.VMEM, pltpu.SemaphoreType.DMA
    any_space = pl.BlockSpec(memory_space=pl.ANY)
    consts = (steering, spectrum, outer_f, outer_i, inner_f, inner_i, twiddle, table, window)
    return pl.pallas_call(
        functools.partial(chain_kernel, (zs, ys, xs, chunks)),
        out_shape=jax.ShapeDtypeStruct((count, pulse_own, gates), F32),
        in_specs=[any_space] * (1 + len(consts)),
        out_specs=pl.BlockSpec(memory_space=vmem),
        scratch_shapes=[vmem(a.shape, a.dtype) for a in consts]
        + [
            vmem((depth, gates), BF),
            vmem((depth, gates), BF),
            vmem((2 * count * beam_rows, gates), BF),
            vmem((2 * count * beam_rows, gates), BF),
            vmem((2 * count * beam_rows, gates), F32),
            vmem((2 * count, beam_rows, gates), BF),
            vmem((ys, xs * beam_rows, gates), BF),
            vmem((ys, xs * beam_rows, gates), BF),
            vmem((xs, ys, gates // LANES * pulse_own, LANES), BF),
            vmem((count, gates // LANES * pulse_own, LANES), BF),
            vmem((2, 2, 2 * count * beam_rows, depth), BF),
            vmem((m_count * 2 * ROWS, m_count * 2 * ROWS), BF),
            vmem((m_count * 2 * ROWS, m_count * 2 * ROWS), BF),
            vmem((2 * pulses, 2 * pulses), BF),
            vmem((4, m_count, ROWS, LANES), F32),
            vmem((2, m_count, LANES), F32),
            dma((len(consts),)),
            dma((chunks,)),
            dma((chunks,)), dma((chunks,)),
            dma((chunks,)), dma((chunks,)),
            dma((chunks,)), dma((chunks,)),
            dma((xs, ys)), dma((count,)),
        ],
        compiler_params=pltpu.CompilerParams(
            collective_id=0, has_side_effects=True, vmem_limit_bytes=VM
        ),
        name="chain",
    )(signal.reshape(depth, gates), *consts)


def shards(signal, steering, spectrum):
    zs, xs, ys = (lax.axis_size(a) for a in ("chan", "pulse", "range"))
    _, _, pulse_own, gates = signal.shape
    fits = (
        zs == 4
        and xs == 4
        and pulse_own == ROWS
        and steering.shape[1] == zs * xs * ys
        and gates * ys * 2 == LANES * LANES
        and gates % (CHUNKS * LANES) == 0
    )
    return (shards_chain if fits else shards_split)(signal, steering, spectrum)


def solution(mesh):
    in_specs = (P(None, "chan", "pulse", "range"), P(), P())
    out_specs = P("chan", "pulse", "range")
    return jax.shard_map(shards, mesh=mesh, in_specs=in_specs, out_specs=out_specs, check_vma=False)
```

time: 97.8 us -> 80.6 us (0.82)
  Pallas kernels: 90.9 us -> 78.2 us
  other arithmetic: 2.25 us -> 0 us
  local copies, waits for them, and re-layouts: 3.84 us -> 2.27 us
    pallas_call x1, Pallas kernels: 90.9 us -> 78.2 us  [shards_chain(): pl.pallas_call(functools.partial(chain_kernel, (zs, ys, xs, chunks)), out...]
where the time goes in v1:
time: 80.6 us; the launch traced here: 80.5 us
  Pallas kernels  78.2 us (97%)
  local copies, waits for them, and re-layouts  2.27 us (3%)
    pallas_call x1, Pallas kernels, shards_chain(): pl.pallas_call(functools.partial(chain_kernel, (zs, ys, xs, chunks)), out...  78.2 us
    unnamed x1, local copies, waits for them, and re-layouts  2.27 us

profile of v1, /device:TPU:0, one launch (start us, length us, event | category | flops | bytes accessed | tf_op | source)
XLA Modules:
  0.0 80.5 jit_solution(8952833310134065715)
XLA Ops:
  0.0 78.2 %chain.1 = f32[8,8,4096]{2,1,0:T(8,128)} custom-call(bf16[256,4096]{1,0:T(8,128)(2,1)} %bitcast.1, bf16[2,32,64]{2,1,0:T(8,128)(2,1)} %steer_h.1, f32[2,8192]{1,0:T(2,128)} %spec_h.1, bf16[128,128]{1,0:T(8,128)(2,1)} %constant.14.clone.f_h, bf16[128,128]{1,0:T(8,128)(2,1)} %constant.15.clone.fi_h, bf16[256,256]{1,0:T(8,128)(2,1)} %constant.16.clone.inf_h, ...), custom_call_target="tpu_custom_call" | custom-call | tf_op jit(solution)/shard_map/chain/pallas_call | solution.py:597
  78.2 2.3 %copy.12 = f32[8,8,4096]{2,1,0:T(8,128)} copy(f32[8,8,4096]{2,1,0:T(8,128)} %chain.1) | data formatting | bytes 2097152

commit v2 on v1

--- a/solution.py
+++ b/solution.py
@@ -15,9 +15,11 @@
 LANES = 128
 ROWS = 8
 CHUNKS = 16
+GROUP = 1
+LAG = 2
 BF = jnp.bfloat16
 F32 = jnp.float32
-VM = 60 * 1024 * 1024
+VM = 44 * 1024 * 1024
 
 
 def dot(a, b):
@@ -285,6 +287,9 @@
     def lanes(c):
         return pl.ds(pl.multiple_of(c * width, LANES), width)
 
+    def wide_lanes(c):
+        return pl.ds(pl.multiple_of(c * width * GROUP, LANES), width * GROUP)
+
     def mine(c):
         return pltpu.make_async_copy(
             sig.at[:, lanes(c)], own1.at[:, lanes(c)], own_sem.at[c]
@@ -363,7 +368,7 @@
 
     def doppler(c):
         for i in range(ys):
-            dop[i, :, lanes(c)] = dot(mix[...], recv2[i, :, lanes(c)]).astype(BF)
+            dop[i, :, wide_lanes(c)] = dot(mix[...], recv2[i, :, wide_lanes(c)]).astype(BF)
 
     @pl.when(is_hub)
     def _():
@@ -403,19 +408,21 @@
             swap(c).wait_recv()
             total = (acc[:, lanes(c)] + recvp[:, lanes(c)].astype(F32)).astype(BF)
             send2[:, :, lanes(c)] = total.reshape(both, beam_rows, width)
+
+        def spray(c):
             mine_rows = pl.ds(pl.multiple_of(beam_rows * x, beam_rows), beam_rows)
             for k in range(1, both):
                 to = lax.rem(me + k, both)
                 plan(
-                    send2.at[to, :, lanes(c)], recv2.at[y, mine_rows, lanes(c)],
+                    send2.at[to, :, wide_lanes(c)], recv2.at[y, mine_rows, wide_lanes(c)],
                     s2.at[c], r2.at[c], plane(to),
                 ).start()
-            recv2[y, mine_rows, lanes(c)] = send2[me, :, lanes(c)]
+            recv2[y, mine_rows, wide_lanes(c)] = send2[me, :, wide_lanes(c)]
 
         def arrived(c):
             plan(
-                send2.at[pl.ds(0, count - 1), :, lanes(c)],
-                send2.at[pl.ds(0, count - 1), :, lanes(c)],
+                send2.at[pl.ds(0, count - 1), :, wide_lanes(c)],
+                send2.at[pl.ds(0, count - 1), :, wide_lanes(c)],
                 s2.at[c], r2.at[c], {"chan": edge},
             ).wait_recv()
 
@@ -426,23 +433,31 @@
             def _():
                 tables()
 
-            @pl.when(c >= 1)
+            @pl.when(c >= LAG)
             def _():
-                finish(c - 1)
-
-            @pl.when(c >= 3)
+                step(c - LAG)
+
+        def step(c):
+            finish(c)
+
+            @pl.when(lax.rem(c, GROUP) == GROUP - 1)
             def _():
-                arrived(c - 3)
-                doppler(c - 3)
+                g = lax.div(c, GROUP)
+                spray(g)
+
+                @pl.when(g >= 3)
+                def _():
+                    arrived(g - 3)
+                    doppler(g - 3)
 
         loop(body)
-        finish(chunks - 1)
+        loop(step, chunks - LAG)
 
         def rest(c):
             arrived(c)
             doppler(c)
 
-        loop(rest, chunks - 3)
+        loop(rest, chunks // GROUP - 3, chunks // GROUP)
 
     @pl.when(is_edge)
     def _():
@@ -450,13 +465,13 @@
 
         def body(c):
             plan(
-                send2.at[pl.ds(0, count), :, lanes(c)],
-                send2.at[pl.ds(0, count), :, lanes(c)],
+                send2.at[pl.ds(0, count), :, wide_lanes(c)],
+                send2.at[pl.ds(0, count), :, wide_lanes(c)],
                 s2.at[c], r2.at[c], {"chan": hub},
             ).wait_recv()
             doppler(c)
 
-        loop(body)
+        loop(body, 0, chunks // GROUP)
 
     tr, ti = spread[0], spread[1]
     hr, hi = spread[2], spread[3]
@@ -543,13 +558,17 @@
                 sendp.at[:, lanes(c)], recvp.at[:, lanes(c)], sp.at[c], rp.at[c],
                 {"chan": 3 - hub},
             ).wait_send()
+
+        loop(body)
+
+        def sprayed(c):
             plan(
-                send2.at[pl.ds(0, both - 1), :, lanes(c)],
-                send2.at[pl.ds(0, both - 1), :, lanes(c)],
+                send2.at[pl.ds(0, both - 1), :, wide_lanes(c)],
+                send2.at[pl.ds(0, both - 1), :, wide_lanes(c)],
                 s2.at[c], r2.at[c], {"chan": edge},
             ).wait_send()
 
-        loop(body)
+        loop(sprayed, 0, chunks // GROUP)
 
 
 def shards_chain(signal, steering, spectrum):
@@ -628,7 +647,10 @@
             collective_id=0, has_side_effects=True, vmem_limit_bytes=VM
         ),
         name="chain",
-    )(signal.reshape(depth, gates), *consts)
+    )(*[
+        pltpu.with_memory_space_constraint(v, pltpu.HBM)
+        for v in (signal.reshape(depth, gates), *map(jnp.asarray, consts))
+    ])
 
 
 def shards(signal, steering, spectrum):

time: 80.6 us -> 77.1 us (0.957)
  Pallas kernels: 78.2 us -> 76 us
  local copies, waits for them, and re-layouts: 2.27 us -> 0.97 us
    pallas_call x1, Pallas kernels: 78.2 us -> 76 us  [shards_chain(): pl.pallas_call(functools.partial(chain_kernel, (zs, ys, xs, chunks)), out...]
    unnamed x1, local copies, waits for them, and re-layouts: 2.27 us -> 0.97 us
where the time goes in v2:
time: 77.1 us; the launch traced here: 77 us
  Pallas kernels  76 us (99%)
  local copies, waits for them, and re-layouts  0.97 us (1%)
    pallas_call x1, Pallas kernels, shards_chain(): pl.pallas_call(functools.partial(chain_kernel, (zs, ys, xs, chunks)), out...  76 us

profile of v2, /device:TPU:0, one launch (start us, length us, event | category | flops | bytes accessed | tf_op | source)
XLA Modules:
  0.0 77.0 jit_solution(5744021666221959007)
XLA Ops:
  0.0 76.0 %chain.1 = f32[8,8,4096]{2,1,0:T(8,128)S(1)} custom-call(bf16[256,4096]{1,0:T(8,128)(2,1)} %bitcast.1, bf16[2,32,64]{2,1,0:T(8,128)(2,1)} %steer_h.1, f32[2,8192]{1,0:T(2,128)} %spec_h.1, bf16[128,128]{1,0:T(8,128)(2,1)} %constant.14.clone.f_h, bf16[128,128]{1,0:T(8,128)(2,1)} %constant.15.clone.fi_h, bf16[256,256]{1,0:T(8,128)(2,1)} %constant.16.clone.inf_h, ...), custom_call_target="tpu_custom_call" | custom-call | tf_op jit(solution)/shard_map/chain/pallas_call | solution.py:616
  76.0 1.0 %copy.12 = f32[8,8,4096]{2,1,0:T(8,128)} copy(f32[8,8,4096]{2,1,0:T(8,128)S(1)} %chain.1) | data formatting | bytes 2097152

commit v3 on v2

--- a/solution.py
+++ b/solution.py
@@ -256,7 +256,7 @@
     sizes, sig, steer_h, spec_h, f_h, fi_h, inf_h, ini_h, tw_h, dop_h, win_h, out,
     steer, spec, f_t, fi_t, inf, ini, tw, dop_t, win,
     own1, recv1, sendp, recvp, acc, send2, recv2, dop, send4, recv4,
-    wide_w, wide_f, wide_i, mix, spread, gates_t,
+    wide_w, mix, resp, gates_t, edges, turn,
     const_sem, own_sem, s1, r1, sp, rp, s2, r2, s4, r4,
 ):
     zs, ys, xs, chunks = sizes
@@ -265,8 +265,10 @@
     beams, chans = steer.shape[1], steer.shape[2]
     count = ys * xs
     beam_rows = send2.shape[1]
-    part_rows = send4.shape[2]
     m_count = tw.shape[1]
+    span = m_count // ys
+    stride = m_count + ROWS
+    turn_row = span + ROWS
     z, y, x = (lax.axis_index(a) for a in ("chan", "range", "pulse"))
     me = y * xs + x
     half = lax.div(z, 2)
@@ -346,18 +348,12 @@
         copy.wait()
 
     def tables():
-        r, c = iota((m_count * 2 * ROWS, 1), 0), iota((1, m_count * 2 * ROWS), 1)
-        ids = (lax.div(r, ROWS), lax.rem(r, ROWS)), (lax.div(c, ROWS), lax.rem(c, ROWS))
-        wide_f[...] = widen(*ids[0], f_t[...], *ids[1])
-        wide_i[...] = widen(*ids[0], fi_t[...], *ids[1])
         for i in range(2):
-            spread[i] = jnp.broadcast_to(tw[i][:, None, :], (m_count, ROWS, LANES))
             for t in range(m_count):
                 gates_t[i, t : t + 1] = spec[i : i + 1, LANES * t : LANES * t + LANES]
             turned = gates_t[i].T * (1.0 / (m_count * LANES))
-            turned = jnp.concatenate([turned[:m_count], turned[m_count:]], axis=1)
-            spread[2 + i] = jnp.broadcast_to(turned[:, None, :], (m_count, ROWS, LANES))
-        chip, core = lax.div(x, 2), lax.rem(x, 2)
+            resp[i] = jnp.concatenate([turned[:m_count], turned[m_count:]], axis=1)
+        edges[...] = jnp.zeros_like(edges)
         for i, g in enumerate(order):
             mix[beam_rows * i : beam_rows * i + beam_rows] = dop_t[
                 pl.ds(pl.multiple_of(beam_rows * g, beam_rows), beam_rows)
@@ -367,8 +363,14 @@
     order = [2 * (1 - chip), 2 * (1 - chip) + 1, 2 * chip + 1 - core, x]
 
     def doppler(c):
+        tiles = width * GROUP // LANES
         for i in range(ys):
-            dop[i, :, wide_lanes(c)] = dot(mix[...], recv2[i, :, wide_lanes(c)]).astype(BF)
+            found = dot(mix[...], recv2[i, :, wide_lanes(c)])
+            for t in range(tiles):
+                m = i * (gates // LANES) + c * tiles + t
+                dop[pl.ds(m, xs * beam_rows, stride=stride)] = found[
+                    :, LANES * t : LANES * t + LANES
+                ]
 
     @pl.when(is_hub)
     def _():
@@ -473,63 +475,82 @@
 
         loop(body, 0, chunks // GROUP)
 
-    tr, ti = spread[0], spread[1]
-    hr, hi = spread[2], spread[3]
+    tr, ti = tw[0], tw[1]
+    hr, hi = resp[0], resp[1]
     fourth = []
-    for q in range(xs // 2):
-        tile = []
-        for j in range(2):
-            rows = slice(beam_rows * (2 * q + j), beam_rows * (2 * q + j + 1))
-            parts = [
-                dop[i, rows, LANES * t : LANES * t + LANES]
-                for i in range(ys)
-                for t in range(gates // LANES)
-            ]
-            tile.append(jnp.concatenate(parts, axis=0))
-        outer = dot(wide_f[...], jnp.concatenate(tile, axis=1))
-        back = []
-        for j in range(2):
-            a = outer[:, LANES * j : LANES * j + LANES].reshape(m_count, 2, ROWS, LANES)
-            ar, ai = a[:, 0], a[:, 1]
-            b = jnp.concatenate([ar * tr - ai * ti, ar * ti + ai * tr], axis=-1)
-            c = dot(b.reshape(m_count * ROWS, 2 * LANES).astype(BF), inf[...])
-            c = c.reshape(m_count, ROWS, 2 * LANES)
-            cr, ci = c[..., :LANES], c[..., LANES:]
-            d = jnp.concatenate([cr * hr - ci * hi, cr * hi + ci * hr], axis=-1)
-            e = dot(d.reshape(m_count * ROWS, 2 * LANES).astype(BF), ini[...])
-            e = e.reshape(m_count, ROWS, 2 * LANES)
-            er, ei = e[..., :LANES], e[..., LANES:]
-            f = jnp.stack([er * tr + ei * ti, ei * tr - er * ti], axis=1)
-            back.append(f.reshape(m_count * 2 * ROWS, LANES).astype(BF))
-        final = dot(wide_i[...], jnp.concatenate(back, axis=1))
-        for j in range(2):
-            v = final[:, LANES * j : LANES * j + LANES].reshape(m_count, 2, ROWS, LANES)
-            re, im = v[:, 0], v[:, 1]
-            power = (re * re + im * im).reshape(m_count * ROWS, LANES)
-            none = jnp.zeros((ROWS, LANES), F32)
-            before = jnp.concatenate([none, power[:-ROWS]], axis=0)
-            after = jnp.concatenate([power[ROWS:], none], axis=0)
-            near = jnp.concatenate([before, power, after], axis=1).astype(BF)
-            found = power / (dot(near, win[...]) + NOISE_FLOOR)
-            p = 2 * q + j
-            send4[p] = found.astype(BF).reshape(send4.shape[1:])
+
+    def split(v, i):
+        w = v[:, LANES * i : LANES * i + LANES]
+        return w[:m_count], w[m_count:]
+
+    def cut(v, i):
+        w = v[m_count * i : m_count * i + m_count]
+        return w[:, :LANES], w[:, LANES:]
+
+    for p in range(xs):
+        cols = []
+        for i in range(ROWS):
+            at = stride * (beam_rows * p + 2 * i)
+            pair = [dop[at : at + m_count], dop[at + stride : at + stride + m_count]]
+            cols.append(jnp.concatenate(pair, axis=0).astype(BF))
+        outer = dot(f_t[...], jnp.concatenate(cols, axis=1))
+        rows = []
+        for i in range(ROWS):
+            ar, ai = split(outer, i)
+            rows.append(
+                jnp.concatenate([ar * tr - ai * ti, ar * ti + ai * tr], axis=1).astype(BF)
+            )
+        inner = dot(jnp.concatenate(rows, axis=0), inf[...])
+        rows = []
+        for i in range(ROWS):
+            cr, ci = cut(inner, i)
+            rows.append(
+                jnp.concatenate([cr * hr - ci * hi, cr * hi + ci * hr], axis=1).astype(BF)
+            )
+        inner = dot(jnp.concatenate(rows, axis=0), ini[...])
+        cols = []
+        for i in range(ROWS):
+            er, ei = cut(inner, i)
+            cols.append(
+                jnp.concatenate([er * tr + ei * ti, ei * tr - er * ti], axis=0).astype(BF)
+            )
+        outer = dot(fi_t[...], jnp.concatenate(cols, axis=1))
+        rows, powers = [], []
+        for i in range(ROWS):
+            re, im = split(outer, i)
+            power = re * re + im * im
+            slot = (p * ROWS + i) % edges.shape[0]
+            edges[slot, ROWS : ROWS + m_count] = power
+            before = edges[slot, ROWS - 1 : ROWS - 1 + m_count]
+            after = edges[slot, ROWS + 1 : ROWS + 1 + m_count]
+            side = jnp.where(iota((m_count, LANES), 1) < LANES // 2, after, before)
+            rows.append(jnp.concatenate([power, side], axis=1).astype(BF))
+            powers.append(power)
+        noise = dot(jnp.concatenate(rows, axis=0), win[...])
+        for i in range(ROWS):
+            level = noise[m_count * i : m_count * i + m_count] + NOISE_FLOOR
+            found = (powers[i] / level).astype(BF)
             for k in range(ys):
-                if p == xs - 1 and k == 0:
-                    recv4[me] = send4[p, y]
-                    continue
-                to_y = lax.rem(y + k, ys)
-                copy = plan(
-                    send4.at[p, to_y], recv4.at[me], s4.at[p, k], r4.at[me],
-                    {"range": to_y, "pulse": order[p]},
-                )
-                copy.start()
-                fourth.append(copy)
+                send4[p, k, span * i : span * i + span] = found[span * k : span * k + span]
+        for k in range(ys):
+            if p == xs - 1 and k == 0:
+                recv4[me] = send4[p, y]
+                continue
+            to_y = lax.rem(y + k, ys)
+            copy = plan(
+                send4.at[p, to_y], recv4.at[me], s4.at[p, k], r4.at[me],
+                {"range": to_y, "pulse": order[p]},
+            )
+            copy.start()
+            fourth.append(copy)
 
     def place(i):
-        for t in range(part_rows // ROWS):
-            out[i, :, LANES * t : LANES * t + LANES] = recv4[
-                i, ROWS * t : ROWS * t + ROWS
+        for b in range(ROWS):
+            turn[turn_row * b : turn_row * b + span] = recv4[
+                i, span * b : span * b + span
             ].astype(F32)
+        for t in range(span):
+            out[i, :, LANES * t : LANES * t + LANES] = turn[pl.ds(t, ROWS, stride=turn_row)]
 
     def final_step(k, carry):
         i = lax.rem(me + k, count)
@@ -584,8 +605,9 @@
 
     ms = np.arange(m_count)
     angle = 2.0 * np.pi * (np.outer(ms, ms) % m_count) / m_count
-    outer_f = jnp.asarray(complex_rows(np.cos(angle), -np.sin(angle)), BF)
-    outer_i = jnp.asarray(complex_rows(np.cos(angle), np.sin(angle)), BF)
+    co, si = np.cos(angle), np.sin(angle)
+    outer_f = jnp.asarray(np.block([[co, si], [-si, co]]), BF)
+    outer_i = jnp.asarray(np.block([[co, -si], [si, co]]), BF)
     ls = np.arange(LANES)
     times = LANES // m_count
     bins = (ls % m_count) * times + ls // m_count
@@ -596,8 +618,9 @@
     angle = 2.0 * np.pi * np.outer(ms, ls) / full
     twiddle = jnp.asarray(np.stack([np.cos(angle), -np.sin(angle)]), F32)
 
-    src, dst = np.arange(3 * LANES)[:, None] - LANES, np.arange(LANES)[None, :]
-    gap = np.abs(src - dst)
+    dst = np.arange(LANES)
+    side = np.where(dst < LANES // 2, dst + LANES, dst - LANES)
+    gap = np.abs(np.concatenate([dst, side])[:, None] - dst[None, :])
     window = jnp.asarray(((gap > GUARD) & (gap <= GUARD + TRAIN)) / (2.0 * TRAIN), BF)
 
     ids = np.arange(pulses)
@@ -606,7 +629,7 @@
     dr, di = np.cos(angle) * scale, -np.sin(angle) * scale
     table = np.stack([np.stack([dr, -di], -1), np.stack([di, dr], -1)])
     table = table.reshape(2, xs, pulse_own, xs, pulse_own, 2)
-    table = table.transpose(1, 0, 2, 3, 5, 4).reshape(2 * pulses, 2 * pulses)
+    table = table.transpose(1, 2, 0, 3, 5, 4).reshape(2 * pulses, 2 * pulses)
     table = jnp.asarray(table, BF)
 
     beam_rows = 2 * pulse_own
@@ -627,15 +650,15 @@
             vmem((2 * count * beam_rows, gates), F32),
             vmem((2 * count, beam_rows, gates), BF),
             vmem((ys, xs * beam_rows, gates), BF),
-            vmem((ys, xs * beam_rows, gates), BF),
+            vmem((xs * beam_rows * (m_count + ROWS), LANES), F32),
             vmem((xs, ys, gates // LANES * pulse_own, LANES), BF),
             vmem((count, gates // LANES * pulse_own, LANES), BF),
             vmem((2, 2, 2 * count * beam_rows, depth), BF),
-            vmem((m_count * 2 * ROWS, m_count * 2 * ROWS), BF),
-            vmem((m_count * 2 * ROWS, m_count * 2 * ROWS), BF),
             vmem((2 * pulses, 2 * pulses), BF),
-            vmem((4, m_count, ROWS, LANES), F32),
             vmem((2, m_count, LANES), F32),
+            vmem((2, m_count, LANES), F32),
+            vmem((2 * ROWS, m_count + 2 * ROWS, LANES), F32),
+            vmem((pulse_own * (m_count // ys + ROWS), LANES), F32),
             dma((len(consts),)),
             dma((chunks,)),
             dma((chunks,)), dma((chunks,)),

time: 77.1 us -> 74.3 us (0.964)
  Pallas kernels: 76 us -> 73.1 us
    pallas_call x1, Pallas kernels: 76 us -> 73.1 us  [shards_chain(): pl.pallas_call(functools.partial(chain_kernel, (zs, ys, xs, chunks)), out...]
where the time goes in v3:
time: 74.3 us; the launch traced here: 74.1 us
  Pallas kernels  73.1 us (98%)
  local copies, waits for them, and re-layouts  0.97 us (1%)
    pallas_call x1, Pallas kernels, shards_chain(): pl.pallas_call(functools.partial(chain_kernel, (zs, ys, xs, chunks)), out...  73.1 us

profile of v3, /device:TPU:0, one launch (start us, length us, event | category | flops | bytes accessed | tf_op | source)
XLA Modules:
  0.0 74.1 jit_solution(6506175800035908218)
XLA Ops:
  0.0 73.1 %chain.1 = f32[8,8,4096]{2,1,0:T(8,128)S(1)} custom-call(bf16[256,4096]{1,0:T(8,128)(2,1)} %bitcast.1, bf16[2,32,64]{2,1,0:T(8,128)(2,1)} %steer_h.1, f32[2,8192]{1,0:T(2,128)} %spec_h.1, bf16[128,128]{1,0:T(8,128)(2,1)} %constant.14.clone.f_h, bf16[128,128]{1,0:T(8,128)(2,1)} %constant.15.clone.fi_h, bf16[256,256]{1,0:T(8,128)(2,1)} %constant.16.clone.inf_h, ...), custom_call_target="tpu_custom_call" | custom-call | tf_op jit(solution)/shard_map/chain/pallas_call | solution.py:639
  73.1 1.0 %copy.12 = f32[8,8,4096]{2,1,0:T(8,128)} copy(f32[8,8,4096]{2,1,0:T(8,128)S(1)} %chain.1) | data formatting | bytes 2097152

commit v4 on v3

--- a/solution.py
+++ b/solution.py
@@ -304,30 +304,30 @@
 
         lax.fori_loop(start, stop, step, 0)
 
+    both = 2 * count
+    barrier = pltpu.get_barrier_semaphore()
+
+    def greet(**target):
+        pl.semaphore_signal(barrier, inc=1, device_id=target, device_id_type=MESH)
+
+    @pl.when(is_hub)
+    def _():
+        greet(chan=edge)
+        for k in range(1, count):
+            to = lax.rem(me + k, count)
+            greet(range=lax.div(to, xs), pulse=lax.rem(to, xs))
+        greet(chan=3 - hub)
+        loop(lambda c: mine(c).start())
+
+    @pl.when(is_edge)
+    def _():
+        for k in range(count):
+            to = lax.rem(me + k, count)
+            greet(chan=hub, range=lax.div(to, xs), pulse=lax.rem(to, xs))
+        pl.semaphore_wait(barrier, 1)
+
     for copy in consts:
         copy.start()
-
-    @pl.when(is_hub)
-    def _():
-        loop(lambda c: mine(c).start())
-
-    def plane(i):
-        d = lax.rem(i, count)
-        return {
-            "chan": jnp.where(i < count, hub, edge),
-            "range": lax.div(d, xs),
-            "pulse": lax.rem(d, xs),
-        }
-
-    both = 2 * count
-    me_both = me + jnp.where(is_hub, 0, count)
-    barrier = pltpu.get_barrier_semaphore()
-    for k in range(1, both):
-        pl.semaphore_signal(
-            barrier, inc=1, device_id=plane(lax.rem(me_both + k, both)), device_id_type=MESH
-        )
-    pl.semaphore_signal(barrier, inc=1, device_id={"chan": 3 - z}, device_id_type=MESH)
-    pl.semaphore_wait(barrier, both)
 
     def plan(src, dst, send, recv, target):
         return pltpu.make_async_remote_copy(
@@ -360,7 +360,16 @@
             ]
 
     chip, core = lax.div(x, 2), lax.rem(x, 2)
-    order = [2 * (1 - chip), 2 * (1 - chip) + 1, 2 * chip + 1 - core, x]
+    order = [2 * (1 - chip) + core, 2 * chip + 1 - core, 2 * (1 - chip) + 1 - core, x]
+
+    hops = sorted(
+        np.ndindex(2, ys, 2, 2), key=lambda k: -(4 * (k[0] + k[1] + k[2]) + k[3])
+    )
+    far_first = [
+        (dz, lax.rem(y + dy, ys), 2 * lax.rem(chip + dx, 2) + lax.rem(core + dc, 2))
+        for dz, dy, dx, dc in hops
+        if (dz, dy, dx, dc) != (0, 0, 0, 0)
+    ]
 
     def doppler(c):
         tiles = width * GROUP // LANES
@@ -413,11 +422,12 @@
 
         def spray(c):
             mine_rows = pl.ds(pl.multiple_of(beam_rows * x, beam_rows), beam_rows)
-            for k in range(1, both):
-                to = lax.rem(me + k, both)
+            for plane_to, to_y, to_x in far_first:
+                to = to_y * xs + to_x
                 plan(
-                    send2.at[to, :, wide_lanes(c)], recv2.at[y, mine_rows, wide_lanes(c)],
-                    s2.at[c], r2.at[c], plane(to),
+                    send2.at[plane_to * count + to, :, wide_lanes(c)],
+                    recv2.at[y, mine_rows, wide_lanes(c)], s2.at[c], r2.at[c],
+                    {"chan": edge if plane_to else hub, "range": to_y, "pulse": to_x},
                 ).start()
             recv2[y, mine_rows, wide_lanes(c)] = send2[me, :, wide_lanes(c)]
 
@@ -427,6 +437,8 @@
                 send2.at[pl.ds(0, count - 1), :, wide_lanes(c)],
                 s2.at[c], r2.at[c], {"chan": edge},
             ).wait_recv()
+
+        pl.semaphore_wait(barrier, both)
 
         def body(c):
             form(c)
@@ -532,7 +544,7 @@
             found = (powers[i] / level).astype(BF)
             for k in range(ys):
                 send4[p, k, span * i : span * i + span] = found[span * k : span * k + span]
-        for k in range(ys):
+        for k in reversed(range(ys)):
             if p == xs - 1 and k == 0:
                 recv4[me] = send4[p, y]
                 continue

time: 74.3 us -> 71.4 us (0.961)
  Pallas kernels: 73.1 us -> 70.2 us
    pallas_call x1, Pallas kernels: 73.1 us -> 70.2 us  [shards_chain(): pl.pallas_call(functools.partial(chain_kernel, (zs, ys, xs, chunks)), out...]
where the time goes in v4:
time: 71.4 us; the launch traced here: 71.1 us
  Pallas kernels  70.2 us (98%)
  local copies, waits for them, and re-layouts  0.97 us (1%)
    pallas_call x1, Pallas kernels, shards_chain(): pl.pallas_call(functools.partial(chain_kernel, (zs, ys, xs, chunks)), out...  70.2 us

profile of v4, /device:TPU:0, one launch (start us, length us, event | category | flops | bytes accessed | tf_op | source)
XLA Modules:
  0.0 71.1 jit_solution(2412001902911804810)
XLA Ops:
  0.0 70.2 %chain.1 = f32[8,8,4096]{2,1,0:T(8,128)S(1)} custom-call(bf16[256,4096]{1,0:T(8,128)(2,1)} %bitcast.1, bf16[2,32,64]{2,1,0:T(8,128)(2,1)} %steer_h.1, f32[2,8192]{1,0:T(2,128)} %spec_h.1, bf16[128,128]{1,0:T(8,128)(2,1)} %constant.14.clone.f_h, bf16[128,128]{1,0:T(8,128)(2,1)} %constant.15.clone.fi_h, bf16[256,256]{1,0:T(8,128)(2,1)} %constant.16.clone.inf_h, ...), custom_call_target="tpu_custom_call" | custom-call | tf_op jit(solution)/shard_map/chain/pallas_call | solution.py:651
  70.2 1.0 %copy.12 = f32[8,8,4096]{2,1,0:T(8,128)} copy(f32[8,8,4096]{2,1,0:T(8,128)S(1)} %chain.1) | data formatting | bytes 2097152

commit v5 on v4

--- a/solution.py
+++ b/solution.py
@@ -15,7 +15,6 @@
 LANES = 128
 ROWS = 8
 CHUNKS = 16
-GROUP = 1
 LAG = 2
 BF = jnp.bfloat16
 F32 = jnp.float32
@@ -255,9 +254,9 @@
 def chain_kernel(
     sizes, sig, steer_h, spec_h, f_h, fi_h, inf_h, ini_h, tw_h, dop_h, win_h, out,
     steer, spec, f_t, fi_t, inf, ini, tw, dop_t, win,
-    own1, recv1, sendp, recvp, acc, send2, recv2, dop, send4, recv4,
+    own1, recv1, sendp, recvp, acc, send2, recv2, recvx, dop, send4, recv4,
     wide_w, mix, resp, gates_t, edges, turn,
-    const_sem, own_sem, s1, r1, sp, rp, s2, r2, s4, r4,
+    const_sem, own_sem, s1, r1, sp, rp, s2, r2, sx, rx, s4, r4,
 ):
     zs, ys, xs, chunks = sizes
     depth, gates = own1.shape
@@ -289,9 +288,6 @@
     def lanes(c):
         return pl.ds(pl.multiple_of(c * width, LANES), width)
 
-    def wide_lanes(c):
-        return pl.ds(pl.multiple_of(c * width * GROUP, LANES), width * GROUP)
-
     def mine(c):
         return pltpu.make_async_copy(
             sig.at[:, lanes(c)], own1.at[:, lanes(c)], own_sem.at[c]
@@ -371,15 +367,24 @@
         if (dz, dy, dx, dc) != (0, 0, 0, 0)
     ]
 
-    def doppler(c):
-        tiles = width * GROUP // LANES
+    def doppler(c, extra=False):
+        tiles = width // LANES
         for i in range(ys):
-            found = dot(mix[...], recv2[i, :, wide_lanes(c)])
+            v = recv2[i, :, lanes(c)]
+            if extra:
+                v = (v.astype(F32) + recvx[i].astype(F32)).astype(BF)
+            found = dot(mix[...], v)
             for t in range(tiles):
                 m = i * (gates // LANES) + c * tiles + t
                 dop[pl.ds(m, xs * beam_rows, stride=stride)] = found[
                     :, LANES * t : LANES * t + LANES
                 ]
+
+    last = chunks - 1
+
+    def doppler_last():
+        plan(recvx, recvx, sx.at[0], rx.at[0], {"chan": 3 - z}).wait_recv()
+        doppler(last, True)
 
     @pl.when(is_hub)
     def _():
@@ -401,9 +406,16 @@
                 col = lax.div(c, chan_own) * chans + source * chan_own + lax.rem(c, chan_own)
                 wide_w[i, j] = widen(row, row_tag, weights, col, col_tag)
 
-        def swap(c):
+        part = count * beam_rows
+        mine_rows = pl.ds(pl.multiple_of(beam_rows * x, beam_rows), beam_rows)
+
+        def rows(u):
+            return slice(part * u, part * u + part)
+
+        def swap(c, u):
+            at = pl.ds(part * u, part)
             return plan(
-                sendp.at[:, lanes(c)], recvp.at[:, lanes(c)], sp.at[c], rp.at[c],
+                sendp.at[at, lanes(c)], recvp.at[at, lanes(c)], sp.at[c, u], rp.at[c, u],
                 {"chan": 3 - hub},
             )
 
@@ -411,30 +423,63 @@
             mine(c).wait()
             raw(c).wait_recv()
             a, b = own1[:, lanes(c)], recv1[:, lanes(c)]
-            sendp[:, lanes(c)] = (dot(wide_w[1, 0], a) + dot(wide_w[1, 1], b)).astype(BF)
-            swap(c).start()
+            for u in (1, 0):
+                far = dot(wide_w[1, 0, rows(u)], a) + dot(wide_w[1, 1, rows(u)], b)
+                sendp[rows(u), lanes(c)] = far.astype(BF)
+                swap(c, u).start()
             acc[:, lanes(c)] = dot(wide_w[0, 0], a) + dot(wide_w[0, 1], b)
 
-        def finish(c):
-            swap(c).wait_recv()
-            total = (acc[:, lanes(c)] + recvp[:, lanes(c)].astype(F32)).astype(BF)
-            send2[:, :, lanes(c)] = total.reshape(both, beam_rows, width)
-
-        def spray(c):
-            mine_rows = pl.ds(pl.multiple_of(beam_rows * x, beam_rows), beam_rows)
+        def spray(c, u):
             for plane_to, to_y, to_x in far_first:
+                if plane_to != u:
+                    continue
                 to = to_y * xs + to_x
                 plan(
-                    send2.at[plane_to * count + to, :, wide_lanes(c)],
-                    recv2.at[y, mine_rows, wide_lanes(c)], s2.at[c], r2.at[c],
+                    send2.at[plane_to * count + to, :, lanes(c)],
+                    recv2.at[y, mine_rows, lanes(c)], s2.at[c], r2.at[c],
                     {"chan": edge if plane_to else hub, "range": to_y, "pulse": to_x},
                 ).start()
-            recv2[y, mine_rows, wide_lanes(c)] = send2[me, :, wide_lanes(c)]
+
+        def finish(c):
+            for u in (1, 0):
+                swap(c, u).wait_recv()
+                total = acc[rows(u), lanes(c)] + recvp[rows(u), lanes(c)].astype(F32)
+                total = total.astype(BF).reshape(count, beam_rows, width)
+                send2[count * u : count * u + count, :, lanes(c)] = total
+                spray(c, u)
+            recv2[y, mine_rows, lanes(c)] = send2[me, :, lanes(c)]
+
+        def form_last():
+            mine(last).wait()
+            raw(last).wait_recv()
+            a, b = own1[:, lanes(last)], recv1[:, lanes(last)]
+            for u in (1, 0):
+                far = dot(wide_w[1, 0, rows(u)], a) + dot(wide_w[1, 1, rows(u)], b)
+                sendp[rows(u), lanes(last)] = far.astype(BF)
+                for plane_to, to_y, to_x in far_first + [(0, y, x)]:
+                    if plane_to != u:
+                        continue
+                    to = plane_to * count + to_y * xs + to_x
+                    at = pl.ds(pl.multiple_of(beam_rows * to, beam_rows), beam_rows)
+                    plan(
+                        sendp.at[at, lanes(last)], recvx.at[y, mine_rows], sx.at[0], rx.at[0],
+                        {
+                            "chan": 3 - edge if plane_to else 3 - hub,
+                            "range": to_y,
+                            "pulse": to_x,
+                        },
+                    ).start()
+            for u in (1, 0):
+                total = dot(wide_w[0, 0, rows(u)], a) + dot(wide_w[0, 1, rows(u)], b)
+                total = total.astype(BF).reshape(count, beam_rows, width)
+                send2[count * u : count * u + count, :, lanes(last)] = total
+                spray(last, u)
+            recv2[y, mine_rows, lanes(last)] = send2[me, :, lanes(last)]
 
         def arrived(c):
             plan(
-                send2.at[pl.ds(0, count - 1), :, wide_lanes(c)],
-                send2.at[pl.ds(0, count - 1), :, wide_lanes(c)],
+                send2.at[pl.ds(0, count - 1), :, lanes(c)],
+                send2.at[pl.ds(0, count - 1), :, lanes(c)],
                 s2.at[c], r2.at[c], {"chan": edge},
             ).wait_recv()
 
@@ -454,38 +499,42 @@
         def step(c):
             finish(c)
 
-            @pl.when(lax.rem(c, GROUP) == GROUP - 1)
+            @pl.when(c >= 3)
             def _():
-                g = lax.div(c, GROUP)
-                spray(g)
-
-                @pl.when(g >= 3)
-                def _():
-                    arrived(g - 3)
-                    doppler(g - 3)
-
-        loop(body)
-        loop(step, chunks - LAG)
+                arrived(c - 3)
+                doppler(c - 3)
+
+        loop(body, 0, last)
+        loop(step, last - LAG, last - 1)
+        form_last()
+        step(last - 1)
 
         def rest(c):
             arrived(c)
             doppler(c)
 
-        loop(rest, chunks // GROUP - 3, chunks // GROUP)
+        loop(rest, last - 3, last)
+        arrived(last)
+        doppler_last()
 
     @pl.when(is_edge)
     def _():
         tables()
 
-        def body(c):
+        def arrived(c):
             plan(
-                send2.at[pl.ds(0, count), :, wide_lanes(c)],
-                send2.at[pl.ds(0, count), :, wide_lanes(c)],
+                send2.at[pl.ds(0, count), :, lanes(c)],
+                send2.at[pl.ds(0, count), :, lanes(c)],
                 s2.at[c], r2.at[c], {"chan": hub},
             ).wait_recv()
+
+        def body(c):
+            arrived(c)
             doppler(c)
 
-        loop(body, 0, chunks // GROUP)
+        loop(body, 0, last)
+        arrived(last)
+        doppler_last()
 
     tr, ti = tw[0], tw[1]
     hr, hi = resp[0], resp[1]
@@ -587,21 +636,27 @@
     @pl.when(is_hub)
     def _():
         def body(c):
-            plan(
-                sendp.at[:, lanes(c)], recvp.at[:, lanes(c)], sp.at[c], rp.at[c],
-                {"chan": 3 - hub},
-            ).wait_send()
-
-        loop(body)
+            for u in range(2):
+                at = pl.ds(count * beam_rows * u, count * beam_rows)
+                plan(
+                    sendp.at[at, lanes(c)], recvp.at[at, lanes(c)], sp.at[c, u], rp.at[c, u],
+                    {"chan": 3 - hub},
+                ).wait_send()
+
+        loop(body, 0, last)
+        plan(
+            sendp.at[:, lanes(last)], sendp.at[:, lanes(last)], sx.at[0], rx.at[0],
+            {"chan": 3 - hub},
+        ).wait_send()
 
         def sprayed(c):
             plan(
-                send2.at[pl.ds(0, both - 1), :, wide_lanes(c)],
-                send2.at[pl.ds(0, both - 1), :, wide_lanes(c)],
+                send2.at[pl.ds(0, both - 1), :, lanes(c)],
+                send2.at[pl.ds(0, both - 1), :, lanes(c)],
                 s2.at[c], r2.at[c], {"chan": edge},
             ).wait_send()
 
-        loop(sprayed, 0, chunks // GROUP)
+        loop(sprayed, 0, chunks)
 
 
 def shards_chain(signal, steering, spectrum):
@@ -662,6 +717,7 @@
             vmem((2 * count * beam_rows, gates), F32),
             vmem((2 * count, beam_rows, gates), BF),
             vmem((ys, xs * beam_rows, gates), BF),
+            vmem((ys, xs * beam_rows, gates // chunks), BF),
             vmem((xs * beam_rows * (m_count + ROWS), LANES), F32),
             vmem((xs, ys, gates // LANES * pulse_own, LANES), BF),
             vmem((count, gates // LANES * pulse_own, LANES), BF),
@@ -674,8 +730,9 @@
             dma((len(consts),)),
             dma((chunks,)),
             dma((chunks,)), dma((chunks,)),
+            dma((chunks, 2)), dma((chunks, 2)),
             dma((chunks,)), dma((chunks,)),
-            dma((chunks,)), dma((chunks,)),
+            dma((1,)), dma((1,)),
             dma((xs, ys)), dma((count,)),
         ],
         compiler_params=pltpu.CompilerParams(

time: 71.4 us -> 69.8 us (0.978)
  Pallas kernels: 70.2 us -> 68.5 us
    pallas_call x1, Pallas kernels: 70.2 us -> 68.5 us  [shards_chain(): pl.pallas_call(functools.partial(chain_kernel, (zs, ys, xs, chunks)), out...]
where the time goes in v5:
time: 69.8 us; the launch traced here: 69.5 us
  Pallas kernels  68.5 us (98%)
  local copies, waits for them, and re-layouts  0.97 us (1%)
    pallas_call x1, Pallas kernels, shards_chain(): pl.pallas_call(functools.partial(chain_kernel, (zs, ys, xs, chunks)), out...  68.5 us

profile of v5, /device:TPU:0, one launch (start us, length us, event | category | flops | bytes accessed | tf_op | source)
XLA Modules:
  0.0 69.5 jit_solution(7472860703536214095)
XLA Ops:
  0.0 68.5 %chain.1 = f32[8,8,4096]{2,1,0:T(8,128)S(1)} custom-call(bf16[256,4096]{1,0:T(8,128)(2,1)} %bitcast.1, bf16[2,32,64]{2,1,0:T(8,128)(2,1)} %steer_h.1, f32[2,8192]{1,0:T(2,128)} %spec_h.1, bf16[128,128]{1,0:T(8,128)(2,1)} %constant.14.clone.f_h, bf16[128,128]{1,0:T(8,128)(2,1)} %constant.15.clone.fi_h, bf16[256,256]{1,0:T(8,128)(2,1)} %constant.16.clone.inf_h, ...), custom_call_target="tpu_custom_call" | custom-call | tf_op jit(solution)/shard_map/chain/pallas_call | solution.py:706
  68.5 1.0 %copy.12 = f32[8,8,4096]{2,1,0:T(8,128)} copy(f32[8,8,4096]{2,1,0:T(8,128)S(1)} %chain.1) | data formatting | bytes 2097152

commit v6 on v5

--- a/solution.py
+++ b/solution.py
@@ -16,6 +16,7 @@
 ROWS = 8
 CHUNKS = 16
 LAG = 2
+DIRECT = 2
 BF = jnp.bfloat16
 F32 = jnp.float32
 VM = 44 * 1024 * 1024
@@ -372,7 +373,7 @@
         for i in range(ys):
             v = recv2[i, :, lanes(c)]
             if extra:
-                v = (v.astype(F32) + recvx[i].astype(F32)).astype(BF)
+                v = (v.astype(F32) + recvx[c - first, i].astype(F32)).astype(BF)
             found = dot(mix[...], v)
             for t in range(tiles):
                 m = i * (gates // LANES) + c * tiles + t
@@ -380,11 +381,12 @@
                     :, LANES * t : LANES * t + LANES
                 ]
 
-    last = chunks - 1
-
-    def doppler_last():
-        plan(recvx, recvx, sx.at[0], rx.at[0], {"chan": 3 - z}).wait_recv()
-        doppler(last, True)
+    first = chunks - DIRECT
+
+    def doppler_both(c):
+        k = c - first
+        plan(recvx.at[k], recvx.at[k], sx.at[k], rx.at[k], {"chan": 3 - z}).wait_recv()
+        doppler(c, True)
 
     @pl.when(is_hub)
     def _():
@@ -449,20 +451,20 @@
                 spray(c, u)
             recv2[y, mine_rows, lanes(c)] = send2[me, :, lanes(c)]
 
-        def form_last():
-            mine(last).wait()
-            raw(last).wait_recv()
-            a, b = own1[:, lanes(last)], recv1[:, lanes(last)]
+        def form_both(c):
+            mine(c).wait()
+            raw(c).wait_recv()
+            a, b = own1[:, lanes(c)], recv1[:, lanes(c)]
             for u in (1, 0):
                 far = dot(wide_w[1, 0, rows(u)], a) + dot(wide_w[1, 1, rows(u)], b)
-                sendp[rows(u), lanes(last)] = far.astype(BF)
+                sendp[rows(u), lanes(c)] = far.astype(BF)
                 for plane_to, to_y, to_x in far_first + [(0, y, x)]:
                     if plane_to != u:
                         continue
                     to = plane_to * count + to_y * xs + to_x
                     at = pl.ds(pl.multiple_of(beam_rows * to, beam_rows), beam_rows)
                     plan(
-                        sendp.at[at, lanes(last)], recvx.at[y, mine_rows], sx.at[0], rx.at[0],
+                        sendp.at[at, lanes(c)], recvx.at[c - first, y, mine_rows], sx.at[c - first], rx.at[c - first],
                         {
                             "chan": 3 - edge if plane_to else 3 - hub,
                             "range": to_y,
@@ -472,9 +474,9 @@
             for u in (1, 0):
                 total = dot(wide_w[0, 0, rows(u)], a) + dot(wide_w[0, 1, rows(u)], b)
                 total = total.astype(BF).reshape(count, beam_rows, width)
-                send2[count * u : count * u + count, :, lanes(last)] = total
-                spray(last, u)
-            recv2[y, mine_rows, lanes(last)] = send2[me, :, lanes(last)]
+                send2[count * u : count * u + count, :, lanes(c)] = total
+                spray(c, u)
+            recv2[y, mine_rows, lanes(c)] = send2[me, :, lanes(c)]
 
         def arrived(c):
             plan(
@@ -504,18 +506,29 @@
                 arrived(c - 3)
                 doppler(c - 3)
 
-        loop(body, 0, last)
-        loop(step, last - LAG, last - 1)
-        form_last()
-        step(last - 1)
+        loop(body, 0, first)
+        step(first - 2)
+
+        def final(c):
+            form_both(c)
+
+            @pl.when(c == first)
+            def _():
+                step(first - 1)
+
+        loop(final, first)
 
         def rest(c):
             arrived(c)
             doppler(c)
 
-        loop(rest, last - 3, last)
-        arrived(last)
-        doppler_last()
+        loop(rest, first - 3, first)
+
+        def rest_both(c):
+            arrived(c)
+            doppler_both(c)
+
+        loop(rest_both, first)
 
     @pl.when(is_edge)
     def _():
@@ -532,9 +545,13 @@
             arrived(c)
             doppler(c)
 
-        loop(body, 0, last)
-        arrived(last)
-        doppler_last()
+        loop(body, 0, first)
+
+        def body_both(c):
+            arrived(c)
+            doppler_both(c)
+
+        loop(body_both, first)
 
     tr, ti = tw[0], tw[1]
     hr, hi = resp[0], resp[1]
@@ -613,22 +630,6 @@
         for t in range(span):
             out[i, :, LANES * t : LANES * t + LANES] = turn[pl.ds(t, ROWS, stride=turn_row)]
 
-    def final_step(k, carry):
-        i = lax.rem(me + k, count)
-
-        @pl.when(k > 0)
-        def _():
-            plan(
-                send4.at[0, 0], recv4.at[i], s4.at[0, 0], r4.at[i], {"chan": 3 - z}
-            ).wait_recv()
-
-        place(i)
-        return carry
-
-    lax.fori_loop(0, count, final_step, 0)
-    for copy in fourth:
-        copy.wait_send()
-
     @pl.when(is_edge)
     def _():
         loop(lambda c: raw(c).wait_send())
@@ -643,11 +644,12 @@
                     {"chan": 3 - hub},
                 ).wait_send()
 
-        loop(body, 0, last)
-        plan(
-            sendp.at[:, lanes(last)], sendp.at[:, lanes(last)], sx.at[0], rx.at[0],
-            {"chan": 3 - hub},
-        ).wait_send()
+        loop(body, 0, first)
+        for k in range(DIRECT):
+            plan(
+                sendp.at[:, lanes(first + k)], sendp.at[:, lanes(first + k)], sx.at[k],
+                rx.at[k], {"chan": 3 - hub},
+            ).wait_send()
 
         def sprayed(c):
             plan(
@@ -657,6 +659,22 @@
             ).wait_send()
 
         loop(sprayed, 0, chunks)
+
+    def from_peer(dy, dx, dc):
+        i = lax.rem(y + dy, ys) * xs + 2 * lax.rem(chip + dx, 2) + lax.rem(core + dc, 2)
+        if (dy, dx, dc) != (0, 0, 0):
+            plan(
+                send4.at[0, 0], recv4.at[i], s4.at[0, 0], r4.at[i], {"chan": 3 - z}
+            ).wait_recv()
+        place(i)
+
+    near_first = sorted(np.ndindex(ys, 2, 2), key=lambda k: (k[1], k[0], k[2]))
+    for k in near_first[:-2]:
+        from_peer(*k)
+    for copy in fourth:
+        copy.wait_send()
+    for k in near_first[-2:]:
+        from_peer(*k)
 
 
 def shards_chain(signal, steering, spectrum):
@@ -717,7 +735,7 @@
             vmem((2 * count * beam_rows, gates), F32),
             vmem((2 * count, beam_rows, gates), BF),
             vmem((ys, xs * beam_rows, gates), BF),
-            vmem((ys, xs * beam_rows, gates // chunks), BF),
+            vmem((DIRECT, ys, xs * beam_rows, gates // chunks), BF),
             vmem((xs * beam_rows * (m_count + ROWS), LANES), F32),
             vmem((xs, ys, gates // LANES * pulse_own, LANES), BF),
             vmem((count, gates // LANES * pulse_own, LANES), BF),
@@ -732,7 +750,7 @@
             dma((chunks,)), dma((chunks,)),
             dma((chunks, 2)), dma((chunks, 2)),
             dma((chunks,)), dma((chunks,)),
-            dma((1,)), dma((1,)),
+            dma((DIRECT,)), dma((DIRECT,)),
             dma((xs, ys)), dma((count,)),
         ],
         compiler_params=pltpu.CompilerParams(

time: 69.8 us -> 69.6 us (level)
  no operation moved by 1% of the time
where the time goes in v6:
time: 69.6 us; the launch traced here: 69.3 us
  Pallas kernels  68.4 us (98%)
  local copies, waits for them, and re-layouts  0.97 us (1%)
    pallas_call x1, Pallas kernels, shards_chain(): pl.pallas_call(functools.partial(chain_kernel, (zs, ys, xs, chunks)), out...  68.4 us

profile of v6, /device:TPU:0, one launch (start us, length us, event | category | flops | bytes accessed | tf_op | source)
XLA Modules:
  0.0 69.3 jit_solution(10334912368457585306)
XLA Ops:
  0.0 68.4 %chain.1 = f32[8,8,4096]{2,1,0:T(8,128)S(1)} custom-call(bf16[256,4096]{1,0:T(8,128)(2,1)} %bitcast.1, bf16[2,32,64]{2,1,0:T(8,128)(2,1)} %steer_h.1, f32[2,8192]{1,0:T(2,128)} %spec_h.1, bf16[128,128]{1,0:T(8,128)(2,1)} %constant.14.clone.f_h, bf16[128,128]{1,0:T(8,128)(2,1)} %constant.15.clone.fi_h, bf16[256,256]{1,0:T(8,128)(2,1)} %constant.16.clone.inf_h, ...), custom_call_target="tpu_custom_call" | custom-call | tf_op jit(solution)/shard_map/chain/pallas_call | solution.py:724
  68.4 1.0 %copy.12 = f32[8,8,4096]{2,1,0:T(8,128)} copy(f32[8,8,4096]{2,1,0:T(8,128)S(1)} %chain.1) | data formatting | bytes 2097152

commit v7 on v6

--- a/solution.py
+++ b/solution.py
@@ -316,16 +316,6 @@
         greet(chan=3 - hub)
         loop(lambda c: mine(c).start())
 
-    @pl.when(is_edge)
-    def _():
-        for k in range(count):
-            to = lax.rem(me + k, count)
-            greet(chan=hub, range=lax.div(to, xs), pulse=lax.rem(to, xs))
-        pl.semaphore_wait(barrier, 1)
-
-    for copy in consts:
-        copy.start()
-
     def plan(src, dst, send, recv, target):
         return pltpu.make_async_remote_copy(
             src_ref=src, dst_ref=dst, send_sem=send, recv_sem=recv,
@@ -339,8 +329,15 @@
 
     @pl.when(is_edge)
     def _():
+        greet(chan=hub)
+        pl.semaphore_wait(barrier, 1)
         loop(lambda c: raw(c).start())
-
+        for k in range(1, count):
+            to = lax.rem(me + k, count)
+            greet(chan=hub, range=lax.div(to, xs), pulse=lax.rem(to, xs))
+
+    for copy in consts:
+        copy.start()
     for copy in consts:
         copy.wait()
 

time: 69.6 us -> 69.6 us (level)
  no operation moved by 1% of the time
where the time goes in v7:
time: 69.6 us; the launch traced here: 69.3 us
  Pallas kernels  68.4 us (98%)
  local copies, waits for them, and re-layouts  0.97 us (1%)
    pallas_call x1, Pallas kernels, shards_chain(): pl.pallas_call(functools.partial(chain_kernel, (zs, ys, xs, chunks)), out...  68.4 us

profile of v7, /device:TPU:0, one launch (start us, length us, event | category | flops | bytes accessed | tf_op | source)
XLA Modules:
  0.0 69.3 jit_solution(1714498239480088510)
XLA Ops:
  0.0 68.4 %chain.1 = f32[8,8,4096]{2,1,0:T(8,128)S(1)} custom-call(bf16[256,4096]{1,0:T(8,128)(2,1)} %bitcast.1, bf16[2,32,64]{2,1,0:T(8,128)(2,1)} %steer_h.1, f32[2,8192]{1,0:T(2,128)} %spec_h.1, bf16[128,128]{1,0:T(8,128)(2,1)} %constant.14.clone.f_h, bf16[128,128]{1,0:T(8,128)(2,1)} %constant.15.clone.fi_h, bf16[256,256]{1,0:T(8,128)(2,1)} %constant.16.clone.inf_h, ...), custom_call_target="tpu_custom_call" | custom-call | tf_op jit(solution)/shard_map/chain/pallas_call | solution.py:721
  68.4 1.0 %copy.12 = f32[8,8,4096]{2,1,0:T(8,128)} copy(f32[8,8,4096]{2,1,0:T(8,128)S(1)} %chain.1) | data formatting | bytes 2097152
